TPU v7x, 32 devices: a 4x4x1 block of a 4x4x8 slice. The times are simulated.
32 devices in a mesh: dp: 1 (over z), cp: 32 (over y, x, core).
Axes of the slice: x: 4, y: 4, z: 1, core: 2. Of those that a mesh axis runs over, the one named last changes fastest.
The devices are a block of a 4x4x8 slice.
Arguments:
- queries: bfloat16 [4, 4096, 8, 256], P('dp', 'cp')
- keys: bfloat16 [4, 4096, 1, 256], P('dp', 'cp')
- values: bfloat16 [4, 4096, 1, 256], P('dp', 'cp')
- out_grad: bfloat16 [4, 4096, 8, 256], P('dp', 'cp')
Outputs:
- output 1: bfloat16 [4, 4096, 8, 256], P('dp', 'cp')
- output 2: float32 [4, 8, 4096], P('dp', None, 'cp')
- output 3: bfloat16 [4, 4096, 8, 256], P('dp', 'cp')
- output 4: bfloat16 [4, 4096, 1, 256], P('dp', 'cp')
- output 5: bfloat16 [4, 4096, 1, 256], P('dp', 'cp')
All inputs are finite; a program needn't handle non-finite values.
Results may differ from a plain program's by a relative error of at most 0.0191514.
Values are sent between devices in bfloat16 or wider.
A program may use at most 768 MiB of HBM per device.

v0:
```python
import jax
import jax.numpy as jnp
from jax import lax
from jax.sharding import PartitionSpec as P


def block_scores(query5, key_blk, scale, causal):
    scores = jnp.einsum("bqgrd,bkgd->bgrqk", query5, key_blk, preferred_element_type=jnp.float32) * scale
    if causal:
        tokens = query5.shape[1]
        row_idx = lax.broadcasted_iota(jnp.int32, (tokens, tokens), 0)
        col_idx = lax.broadcasted_iota(jnp.int32, (tokens, tokens), 1)
        scores = jnp.where(row_idx >= col_idx, scores, -jnp.inf)
    return scores


def forward_step(query5, key_blk, value_blk, state, scale, causal):
    run_max, run_sum, run_acc = state
    scores = block_scores(query5, key_blk, scale, causal)
    new_max = jnp.maximum(run_max, jnp.max(scores, axis=-1))
    alpha = jnp.exp(run_max - new_max)
    weights = jnp.exp(scores - new_max[..., None])
    new_sum = run_sum * alpha + jnp.sum(weights, axis=-1)
    new_acc = run_acc * alpha[..., None] + jnp.einsum("bgrqk,bkgd->bgrqd", weights.astype(jnp.bfloat16), value_blk, preferred_element_type=jnp.float32)
    return new_max, new_sum, new_acc


def backward_step(query5, grad5, row_lse, delta, key_blk, value_blk, scale, causal):
    scores = block_scores(query5, key_blk, scale, causal)
    prob_mat = jnp.exp(scores - row_lse[..., None])
    grad_prob = jnp.einsum("bqgrd,bkgd->bgrqk", grad5, value_blk, preferred_element_type=jnp.float32)
    grad_score = (prob_mat * (grad_prob - delta[..., None])).astype(jnp.bfloat16)
    prob_low = prob_mat.astype(jnp.bfloat16)
    dq_part = jnp.einsum("bgrqk,bkgd->bqgrd", grad_score, key_blk, preferred_element_type=jnp.float32) * scale
    dk_part = jnp.einsum("bgrqk,bqgrd->bkgd", grad_score, query5, preferred_element_type=jnp.float32) * scale
    dv_part = jnp.einsum("bgrqk,bqgrd->bkgd", prob_low, grad5, preferred_element_type=jnp.float32)
    return dq_part, dk_part, dv_part


def solution(mesh):
    cp_size = mesh.shape["cp"]
    shift_pairs = [(source, (source + 1) % cp_size) for source in range(cp_size)]

    def attention_shard(queries, keys, values, out_grad):
        batch, tokens, heads, head_dim = queries.shape
        kv_heads = keys.shape[2]
        ratio = heads // kv_heads
        scale = head_dim ** -0.5
        cp_rank = lax.axis_index("cp")
        query5 = queries.reshape(batch, tokens, kv_heads, ratio, head_dim)
        grad5 = out_grad.reshape(batch, tokens, kv_heads, ratio, head_dim)
        stat_shape = (batch, kv_heads, ratio, tokens)
        init_state = (jnp.full(stat_shape, -jnp.inf, jnp.float32), jnp.zeros(stat_shape, jnp.float32), jnp.zeros(stat_shape + (head_dim,), jnp.float32))
        diag_state = forward_step(query5, keys, values, init_state, scale, True)

        def forward_body(step, carry):
            key_cur, value_cur, state = carry
            key_cur = lax.ppermute(key_cur, "cp", shift_pairs)
            value_cur = lax.ppermute(value_cur, "cp", shift_pairs)
            state = lax.cond(step <= cp_rank, lambda prev: forward_step(query5, key_cur, value_cur, prev, scale, False), lambda prev: prev, state)
            return key_cur, value_cur, state

        run_max, run_sum, run_acc = lax.fori_loop(1, cp_size, forward_body, (keys, values, diag_state))[2]
        out5 = (run_acc / run_sum[..., None]).astype(jnp.bfloat16)
        attn_out = jnp.transpose(out5, (0, 3, 1, 2, 4)).reshape(batch, tokens, heads, head_dim)
        row_lse = run_max + jnp.log(run_sum)
        delta = jnp.einsum("bqgrd,bgrqd->bgrq", grad5, out5, preferred_element_type=jnp.float32)

        dq_diag, dk_diag, dv_diag = backward_step(query5, grad5, row_lse, delta, keys, values, scale, True)

        def backward_body(step, carry):
            key_cur, value_cur, dk_cur, dv_cur, dq_acc = carry
            key_cur = lax.ppermute(key_cur, "cp", shift_pairs)
            value_cur = lax.ppermute(value_cur, "cp", shift_pairs)
            dk_cur = lax.ppermute(dk_cur, "cp", shift_pairs)
            dv_cur = lax.ppermute(dv_cur, "cp", shift_pairs)

            def visit(acc_in):
                dk_in, dv_in, dq_in = acc_in
                dq_part, dk_part, dv_part = backward_step(query5, grad5, row_lse, delta, key_cur, value_cur, scale, False)
                return dk_in + dk_part, dv_in + dv_part, dq_in + dq_part

            dk_cur, dv_cur, dq_acc = lax.cond(step <= cp_rank, visit, lambda acc_in: acc_in, (dk_cur, dv_cur, dq_acc))
            return key_cur, value_cur, dk_cur, dv_cur, dq_acc

        carry_out = lax.fori_loop(1, cp_size, backward_body, (keys, values, dk_diag, dv_diag, dq_diag))
        dk_home = lax.ppermute(carry_out[2], "cp", shift_pairs)
        dv_home = lax.ppermute(carry_out[3], "cp", shift_pairs)
        grad_query = carry_out[4].reshape(batch, tokens, heads, head_dim).astype(jnp.bfloat16)
        return attn_out, row_lse.reshape(batch, heads, tokens), grad_query, dk_home.astype(jnp.bfloat16), dv_home.astype(jnp.bfloat16)

    seq_spec = P("dp", "cp")
    return jax.shard_map(attention_shard, mesh=mesh, in_specs=(seq_spec, seq_spec, seq_spec, seq_spec), out_specs=(seq_spec, P("dp", None, "cp"), seq_spec, seq_spec, seq_spec), check_vma=False)
```

profile of v0, /device:TPU:120, one launch (start us, length us, event | category | flops | bytes accessed | tf_op | source)
XLA Modules:
  0.0 1497.9 jit_solution(9825373234696420587)
XLA Ops:
  15.9 476.8 %while.42 = (s32[]{:T(128)}, bf16[4,128,1,256]{3,1,0,2:T(8,128)(2,1)S(1)}, bf16[4,128,1,256]{3,1,0,2:T(8,128)(2,1)S(1)}, f32[4,1,8,128]{3,2,0,1:T(8,128)S(1)}, f...) while((s32[]{:T(128)}, ...), condition=%wide.region_7.8_spmd, body=%wide.region_2.7_spmd.sunk | while | flops 543174656 | bytes 54264152 | solution.py:63
  32.7 7.8 collective-permute-done.1
  49.4 7.8 collective-permute-done.1
  82.8 7.8 collective-permute-done.1
  99.5 7.8 collective-permute-done.1
  132.9 7.8 collective-permute-done.1
  149.6 7.8 collective-permute-done.1
  166.3 7.8 collective-permute-done.1
  510.8 973.8 %while.43 = (s32[]{:T(128)}, bf16[4,128,1,256]{3,1,0,2:T(8,128)(2,1)}, bf16[4,128,1,256]{3,1,0,2:T(8,128)(2,1)}, f32[4,128,1,256]{3,1,0,2:T(8,128)}, f32[4,128,1...) while((s32[]{:T(128)}, ...), condition=%wide.region_11.12_spmd, body=%wide.region_8.11_spmd.sunk | while | flops 1348861952 | bytes 80527856 | solution.py:86
  510.9 19.0 %collective-permute-done.3 = bf16[4,128,1,256]{3,1,0,2:T(8,128)(2,1)} collective-permute-done((bf16[4,128,1,256]{3,1,0,2:T(8,128)(2,1)}, bf16[4,128,1,256]{3,1,0,2:T(8,128)(2,1)}, u32[]{:S(2)}, u32[]{:S(2)}) %collective-permute-start.3) | collective-permute-done | bytes 262176 | tf_op jit(solution)/shard_map/while/body/eval_jaxpr/ppermute | solution.py:74
  533.4 9.2 conditional.5
  544.4 19.0 %collective-permute-done.3 = bf16[4,128,1,256]{3,1,0,2:T(8,128)(2,1)} collective-permute-done((bf16[4,128,1,256]{3,1,0,2:T(8,128)(2,1)}, bf16[4,128,1,256]{3,1,0,2:T(8,128)(2,1)}, u32[]{:S(2)}, u32[]{:S(2)}) %collective-permute-start.3) | collective-permute-done | bytes 262176 | tf_op jit(solution)/shard_map/while/body/eval_jaxpr/ppermute | solution.py:74
  566.9 9.2 conditional.5
  577.9 19.0 %collective-permute-done.3 = bf16[4,128,1,256]{3,1,0,2:T(8,128)(2,1)} collective-permute-done((bf16[4,128,1,256]{3,1,0,2:T(8,128)(2,1)}, bf16[4,128,1,256]{3,1,0,2:T(8,128)(2,1)}, u32[]{:S(2)}, u32[]{:S(2)}) %collective-permute-start.3) | collective-permute-done | bytes 262176 | tf_op jit(solution)/shard_map/while/body/eval_jaxpr/ppermute | solution.py:74
  600.4 9.2 conditional.5
  611.4 19.0 %collective-permute-done.3 = bf16[4,128,1,256]{3,1,0,2:T(8,128)(2,1)} collective-permute-done((bf16[4,128,1,256]{3,1,0,2:T(8,128)(2,1)}, bf16[4,128,1,256]{3,1,0,2:T(8,128)(2,1)}, u32[]{:S(2)}, u32[]{:S(2)}) %collective-permute-start.3) | collective-permute-done | bytes 262176 | tf_op jit(solution)/shard_map/while/body/eval_jaxpr/ppermute | solution.py:74
  633.9 9.2 conditional.5
  644.9 19.0 %collective-permute-done.3 = bf16[4,128,1,256]{3,1,0,2:T(8,128)(2,1)} collective-permute-done((bf16[4,128,1,256]{3,1,0,2:T(8,128)(2,1)}, bf16[4,128,1,256]{3,1,0,2:T(8,128)(2,1)}, u32[]{:S(2)}, u32[]{:S(2)}) %collective-permute-start.3) | collective-permute-done | bytes 262176 | tf_op jit(solution)/shard_map/while/body/eval_jaxpr/ppermute | solution.py:74
  667.4 9.2 conditional.5
  678.4 19.0 %collective-permute-done.3 = bf16[4,128,1,256]{3,1,0,2:T(8,128)(2,1)} collective-permute-done((bf16[4,128,1,256]{3,1,0,2:T(8,128)(2,1)}, bf16[4,128,1,256]{3,1,0,2:T(8,128)(2,1)}, u32[]{:S(2)}, u32[]{:S(2)}) %collective-permute-start.3) | collective-permute-done | bytes 262176 | tf_op jit(solution)/shard_map/while/body/eval_jaxpr/ppermute | solution.py:74
  700.9 9.2 conditional.5
  711.9 19.0 %collective-permute-done.3 = bf16[4,128,1,256]{3,1,0,2:T(8,128)(2,1)} collective-permute-done((bf16[4,128,1,256]{3,1,0,2:T(8,128)(2,1)}, bf16[4,128,1,256]{3,1,0,2:T(8,128)(2,1)}, u32[]{:S(2)}, u32[]{:S(2)}) %collective-permute-start.3) | collective-permute-done | bytes 262176 | tf_op jit(solution)/shard_map/while/body/eval_jaxpr/ppermute | solution.py:74
  734.4 9.2 conditional.5
  745.4 19.0 %collective-permute-done.3 = bf16[4,128,1,256]{3,1,0,2:T(8,128)(2,1)} collective-permute-done((bf16[4,128,1,256]{3,1,0,2:T(8,128)(2,1)}, bf16[4,128,1,256]{3,1,0,2:T(8,128)(2,1)}, u32[]{:S(2)}, u32[]{:S(2)}) %collective-permute-start.3) | collective-permute-done | bytes 262176 | tf_op jit(solution)/shard_map/while/body/eval_jaxpr/ppermute | solution.py:74
  767.9 9.2 conditional.5
  778.9 19.0 %collective-permute-done.3 = bf16[4,128,1,256]{3,1,0,2:T(8,128)(2,1)} collective-permute-done((bf16[4,128,1,256]{3,1,0,2:T(8,128)(2,1)}, bf16[4,128,1,256]{3,1,0,2:T(8,128)(2,1)}, u32[]{:S(2)}, u32[]{:S(2)}) %collective-permute-start.3) | collective-permute-done | bytes 262176 | tf_op jit(solution)/shard_map/while/body/eval_jaxpr/ppermute | solution.py:74
  801.4 9.2 conditional.5
  812.4 19.0 %collective-permute-done.3 = bf16[4,128,1,256]{3,1,0,2:T(8,128)(2,1)} collective-permute-done((bf16[4,128,1,256]{3,1,0,2:T(8,128)(2,1)}, bf16[4,128,1,256]{3,1,0,2:T(8,128)(2,1)}, u32[]{:S(2)}, u32[]{:S(2)}) %collective-permute-start.3) | collective-permute-done | bytes 262176 | tf_op jit(solution)/shard_map/while/body/eval_jaxpr/ppermute | solution.py:74
  834.9 9.2 conditional.5
  845.9 19.0 %collective-permute-done.3 = bf16[4,128,1,256]{3,1,0,2:T(8,128)(2,1)} collective-permute-done((bf16[4,128,1,256]{3,1,0,2:T(8,128)(2,1)}, bf16[4,128,1,256]{3,1,0,2:T(8,128)(2,1)}, u32[]{:S(2)}, u32[]{:S(2)}) %collective-permute-start.3) | collective-permute-done | bytes 262176 | tf_op jit(solution)/shard_map/while/body/eval_jaxpr/ppermute | solution.py:74
  868.4 9.2 conditional.5
  879.4 19.0 %collective-permute-done.3 = bf16[4,128,1,256]{3,1,0,2:T(8,128)(2,1)} collective-permute-done((bf16[4,128,1,256]{3,1,0,2:T(8,128)(2,1)}, bf16[4,128,1,256]{3,1,0,2:T(8,128)(2,1)}, u32[]{:S(2)}, u32[]{:S(2)}) %collective-permute-start.3) | collective-permute-done | bytes 262176 | tf_op jit(solution)/shard_map/while/body/eval_jaxpr/ppermute | solution.py:74
  901.9 9.2 conditional.5
  912.9 19.0 %collective-permute-done.3 = bf16[4,128,1,256]{3,1,0,2:T(8,128)(2,1)} collective-permute-done((bf16[4,128,1,256]{3,1,0,2:T(8,128)(2,1)}, bf16[4,128,1,256]{3,1,0,2:T(8,128)(2,1)}, u32[]{:S(2)}, u32[]{:S(2)}) %collective-permute-start.3) | collective-permute-done | bytes 262176 | tf_op jit(solution)/shard_map/while/body/eval_jaxpr/ppermute | solution.py:74
  935.4 9.2 conditional.5
  946.4 19.0 %collective-permute-done.3 = bf16[4,128,1,256]{3,1,0,2:T(8,128)(2,1)} collective-permute-done((bf16[4,128,1,256]{3,1,0,2:T(8,128)(2,1)}, bf16[4,128,1,256]{3,1,0,2:T(8,128)(2,1)}, u32[]{:S(2)}, u32[]{:S(2)}) %collective-permute-start.3) | collective-permute-done | bytes 262176 | tf_op jit(solution)/shard_map/while/body/eval_jaxpr/ppermute | solution.py:74
  968.9 9.2 conditional.5
  979.9 19.0 %collective-permute-done.3 = bf16[4,128,1,256]{3,1,0,2:T(8,128)(2,1)} collective-permute-done((bf16[4,128,1,256]{3,1,0,2:T(8,128)(2,1)}, bf16[4,128,1,256]{3,1,0,2:T(8,128)(2,1)}, u32[]{:S(2)}, u32[]{:S(2)}) %collective-permute-start.3) | collective-permute-done | bytes 262176 | tf_op jit(solution)/shard_map/while/body/eval_jaxpr/ppermute | solution.py:74
  1002.4 9.2 conditional.5
  1013.4 19.0 %collective-permute-done.3 = bf16[4,128,1,256]{3,1,0,2:T(8,128)(2,1)} collective-permute-done((bf16[4,128,1,256]{3,1,0,2:T(8,128)(2,1)}, bf16[4,128,1,256]{3,1,0,2:T(8,128)(2,1)}, u32[]{:S(2)}, u32[]{:S(2)}) %collective-permute-start.3) | collective-permute-done | bytes 262176 | tf_op jit(solution)/shard_map/while/body/eval_jaxpr/ppermute | solution.py:74
  1035.9 9.2 conditional.5
  1046.9 19.0 %collective-permute-done.3 = bf16[4,128,1,256]{3,1,0,2:T(8,128)(2,1)} collective-permute-done((bf16[4,128,1,256]{3,1,0,2:T(8,128)(2,1)}, bf16[4,128,1,256]{3,1,0,2:T(8,128)(2,1)}, u32[]{:S(2)}, u32[]{:S(2)}) %collective-permute-start.3) | collective-permute-done | bytes 262176 | tf_op jit(solution)/shard_map/while/body/eval_jaxpr/ppermute | solution.py:74
  1069.4 9.2 conditional.5
  1080.4 19.0 %collective-permute-done.3 = bf16[4,128,1,256]{3,1,0,2:T(8,128)(2,1)} collective-permute-done((bf16[4,128,1,256]{3,1,0,2:T(8,128)(2,1)}, bf16[4,128,1,256]{3,1,0,2:T(8,128)(2,1)}, u32[]{:S(2)}, u32[]{:S(2)}) %collective-permute-start.3) | collective-permute-done | bytes 262176 | tf_op jit(solution)/shard_map/while/body/eval_jaxpr/ppermute | solution.py:74
  1102.9 9.2 conditional.5
  1113.9 19.0 %collective-permute-done.3 = bf16[4,128,1,256]{3,1,0,2:T(8,128)(2,1)} collective-permute-done((bf16[4,128,1,256]{3,1,0,2:T(8,128)(2,1)}, bf16[4,128,1,256]{3,1,0,2:T(8,128)(2,1)}, u32[]{:S(2)}, u32[]{:S(2)}) %collective-permute-start.3) | collective-permute-done | bytes 262176 | tf_op jit(solution)/shard_map/while/body/eval_jaxpr/ppermute | solution.py:74
  1136.4 9.2 conditional.5
  1147.4 19.0 %collective-permute-done.3 = bf16[4,128,1,256]{3,1,0,2:T(8,128)(2,1)} collective-permute-done((bf16[4,128,1,256]{3,1,0,2:T(8,128)(2,1)}, bf16[4,128,1,256]{3,1,0,2:T(8,128)(2,1)}, u32[]{:S(2)}, u32[]{:S(2)}) %collective-permute-start.3) | collective-permute-done | bytes 262176 | tf_op jit(solution)/shard_map/while/body/eval_jaxpr/ppermute | solution.py:74
  1169.9 9.2 conditional.5
  1180.9 19.0 %collective-permute-done.3 = bf16[4,128,1,256]{3,1,0,2:T(8,128)(2,1)} collective-permute-done((bf16[4,128,1,256]{3,1,0,2:T(8,128)(2,1)}, bf16[4,128,1,256]{3,1,0,2:T(8,128)(2,1)}, u32[]{:S(2)}, u32[]{:S(2)}) %collective-permute-start.3) | collective-permute-done | bytes 262176 | tf_op jit(solution)/shard_map/while/body/eval_jaxpr/ppermute | solution.py:74
  1203.4 9.2 conditional.5
  1214.4 19.0 %collective-permute-done.3 = bf16[4,128,1,256]{3,1,0,2:T(8,128)(2,1)} collective-permute-done((bf16[4,128,1,256]{3,1,0,2:T(8,128)(2,1)}, bf16[4,128,1,256]{3,1,0,2:T(8,128)(2,1)}, u32[]{:S(2)}, u32[]{:S(2)}) %collective-permute-start.3) | collective-permute-done | bytes 262176 | tf_op jit(solution)/shard_map/while/body/eval_jaxpr/ppermute | solution.py:74
  1236.9 9.2 conditional.5
  1247.9 19.0 %collective-permute-done.3 = bf16[4,128,1,256]{3,1,0,2:T(8,128)(2,1)} collective-permute-done((bf16[4,128,1,256]{3,1,0,2:T(8,128)(2,1)}, bf16[4,128,1,256]{3,1,0,2:T(8,128)(2,1)}, u32[]{:S(2)}, u32[]{:S(2)}) %collective-permute-start.3) | collective-permute-done | bytes 262176 | tf_op jit(solution)/shard_map/while/body/eval_jaxpr/ppermute | solution.py:74
  1270.4 9.2 conditional.5
  1281.4 19.0 %collective-permute-done.3 = bf16[4,128,1,256]{3,1,0,2:T(8,128)(2,1)} collective-permute-done((bf16[4,128,1,256]{3,1,0,2:T(8,128)(2,1)}, bf16[4,128,1,256]{3,1,0,2:T(8,128)(2,1)}, u32[]{:S(2)}, u32[]{:S(2)}) %collective-permute-start.3) | collective-permute-done | bytes 262176 | tf_op jit(solution)/shard_map/while/body/eval_jaxpr/ppermute | solution.py:74
  1303.9 9.2 conditional.5
  1314.9 19.0 %collective-permute-done.3 = bf16[4,128,1,256]{3,1,0,2:T(8,128)(2,1)} collective-permute-done((bf16[4,128,1,256]{3,1,0,2:T(8,128)(2,1)}, bf16[4,128,1,256]{3,1,0,2:T(8,128)(2,1)}, u32[]{:S(2)}, u32[]{:S(2)}) %collective-permute-start.3) | collective-permute-done | bytes 262176 | tf_op jit(solution)/shard_map/while/body/eval_jaxpr/ppermute | solution.py:74
  1339.1 19.0 %collective-permute-done.3 = bf16[4,128,1,256]{3,1,0,2:T(8,128)(2,1)} collective-permute-done((bf16[4,128,1,256]{3,1,0,2:T(8,128)(2,1)}, bf16[4,128,1,256]{3,1,0,2:T(8,128)(2,1)}, u32[]{:S(2)}, u32[]{:S(2)}) %collective-permute-start.3) | collective-permute-done | bytes 262176 | tf_op jit(solution)/shard_map/while/body/eval_jaxpr/ppermute | solution.py:74
  1363.4 19.0 %collective-permute-done.3 = bf16[4,128,1,256]{3,1,0,2:T(8,128)(2,1)} collective-permute-done((bf16[4,128,1,256]{3,1,0,2:T(8,128)(2,1)}, bf16[4,128,1,256]{3,1,0,2:T(8,128)(2,1)}, u32[]{:S(2)}, u32[]{:S(2)}) %collective-permute-start.3) | collective-permute-done | bytes 262176 | tf_op jit(solution)/shard_map/while/body/eval_jaxpr/ppermute | solution.py:74
  1387.7 19.0 %collective-permute-done.3 = bf16[4,128,1,256]{3,1,0,2:T(8,128)(2,1)} collective-permute-done((bf16[4,128,1,256]{3,1,0,2:T(8,128)(2,1)}, bf16[4,128,1,256]{3,1,0,2:T(8,128)(2,1)}, u32[]{:S(2)}, u32[]{:S(2)}) %collective-permute-start.3) | collective-permute-done | bytes 262176 | tf_op jit(solution)/shard_map/while/body/eval_jaxpr/ppermute | solution.py:74
  1411.9 19.0 %collective-permute-done.3 = bf16[4,128,1,256]{3,1,0,2:T(8,128)(2,1)} collective-permute-done((bf16[4,128,1,256]{3,1,0,2:T(8,128)(2,1)}, bf16[4,128,1,256]{3,1,0,2:T(8,128)(2,1)}, u32[]{:S(2)}, u32[]{:S(2)}) %collective-permute-start.3) | collective-permute-done | bytes 262176 | tf_op jit(solution)/shard_map/while/body/eval_jaxpr/ppermute | solution.py:74
  1436.2 19.0 %collective-permute-done.3 = bf16[4,128,1,256]{3,1,0,2:T(8,128)(2,1)} collective-permute-done((bf16[4,128,1,256]{3,1,0,2:T(8,128)(2,1)}, bf16[4,128,1,256]{3,1,0,2:T(8,128)(2,1)}, u32[]{:S(2)}, u32[]{:S(2)}) %collective-permute-start.3) | collective-permute-done | bytes 262176 | tf_op jit(solution)/shard_map/while/body/eval_jaxpr/ppermute | solution.py:74
  1460.5 19.0 %collective-permute-done.3 = bf16[4,128,1,256]{3,1,0,2:T(8,128)(2,1)} collective-permute-done((bf16[4,128,1,256]{3,1,0,2:T(8,128)(2,1)}, bf16[4,128,1,256]{3,1,0,2:T(8,128)(2,1)}, u32[]{:S(2)}, u32[]{:S(2)}) %collective-permute-start.3) | collective-permute-done | bytes 262176 | tf_op jit(solution)/shard_map/while/body/eval_jaxpr/ppermute | solution.py:74
  (1104 shorter events, 989.0 us)
Async XLA Ops:
  510.8 22.7 %collective-permute-start.5 = (f32[4,128,1,256]{3,1,0,2:T(8,128)}, f32[4,128,1,256]{3,1,0,2:T(8,128)S(1)}, u32[]{:S(2)}, u32[]{:S(2)}) collective-permute-start(f32[4,128,1,256]{3,1,0,2:T(8,128)} %get-tuple-element.663), channel_id=1, source_target_pairs={{0,1},{1,2},{2,3},{3,4},{4,5},{5,6},{6,7},{7,8},{8,9},{9,10},{10,1... | collective-permute-start | bytes 1572872 | tf_op jit(solution)/shard_map/while/body/eval_jaxpr/ppermute | solution.py:76
  510.8 22.7 %collective-permute-start.4 = (f32[4,128,1,256]{3,1,0,2:T(8,128)}, f32[4,128,1,256]{3,1,0,2:T(8,128)S(1)}, u32[]{:S(2)}, u32[]{:S(2)}) collective-permute-start(f32[4,128,1,256]{3,1,0,2:T(8,128)} %get-tuple-element.662), channel_id=1, source_target_pairs={{0,1},{1,2},{2,3},{3,4},{4,5},{5,6},{6,7},{7,8},{8,9},{9,10},{10,1... | collective-permute-start | bytes 1572872 | tf_op jit(solution)/shard_map/while/body/eval_jaxpr/ppermute | solution.py:75
  544.3 22.7 %collective-permute-start.5 = (f32[4,128,1,256]{3,1,0,2:T(8,128)}, f32[4,128,1,256]{3,1,0,2:T(8,128)S(1)}, u32[]{:S(2)}, u32[]{:S(2)}) collective-permute-start(f32[4,128,1,256]{3,1,0,2:T(8,128)} %get-tuple-element.663), channel_id=1, source_target_pairs={{0,1},{1,2},{2,3},{3,4},{4,5},{5,6},{6,7},{7,8},{8,9},{9,10},{10,1... | collective-permute-start | bytes 1572872 | tf_op jit(solution)/shard_map/while/body/eval_jaxpr/ppermute | solution.py:76
  544.3 22.7 %collective-permute-start.4 = (f32[4,128,1,256]{3,1,0,2:T(8,128)}, f32[4,128,1,256]{3,1,0,2:T(8,128)S(1)}, u32[]{:S(2)}, u32[]{:S(2)}) collective-permute-start(f32[4,128,1,256]{3,1,0,2:T(8,128)} %get-tuple-element.662), channel_id=1, source_target_pairs={{0,1},{1,2},{2,3},{3,4},{4,5},{5,6},{6,7},{7,8},{8,9},{9,10},{10,1... | collective-permute-start | bytes 1572872 | tf_op jit(solution)/shard_map/while/body/eval_jaxpr/ppermute | solution.py:75
  577.8 22.7 %collective-permute-start.5 = (f32[4,128,1,256]{3,1,0,2:T(8,128)}, f32[4,128,1,256]{3,1,0,2:T(8,128)S(1)}, u32[]{:S(2)}, u32[]{:S(2)}) collective-permute-start(f32[4,128,1,256]{3,1,0,2:T(8,128)} %get-tuple-element.663), channel_id=1, source_target_pairs={{0,1},{1,2},{2,3},{3,4},{4,5},{5,6},{6,7},{7,8},{8,9},{9,10},{10,1... | collective-permute-start | bytes 1572872 | tf_op jit(solution)/shard_map/while/body/eval_jaxpr/ppermute | solution.py:76
  577.8 22.7 %collective-permute-start.4 = (f32[4,128,1,256]{3,1,0,2:T(8,128)}, f32[4,128,1,256]{3,1,0,2:T(8,128)S(1)}, u32[]{:S(2)}, u32[]{:S(2)}) collective-permute-start(f32[4,128,1,256]{3,1,0,2:T(8,128)} %get-tuple-element.662), channel_id=1, source_target_pairs={{0,1},{1,2},{2,3},{3,4},{4,5},{5,6},{6,7},{7,8},{8,9},{9,10},{10,1... | collective-permute-start | bytes 1572872 | tf_op jit(solution)/shard_map/while/body/eval_jaxpr/ppermute | solution.py:75
  611.3 22.7 %collective-permute-start.5 = (f32[4,128,1,256]{3,1,0,2:T(8,128)}, f32[4,128,1,256]{3,1,0,2:T(8,128)S(1)}, u32[]{:S(2)}, u32[]{:S(2)}) collective-permute-start(f32[4,128,1,256]{3,1,0,2:T(8,128)} %get-tuple-element.663), channel_id=1, source_target_pairs={{0,1},{1,2},{2,3},{3,4},{4,5},{5,6},{6,7},{7,8},{8,9},{9,10},{10,1... | collective-permute-start | bytes 1572872 | tf_op jit(solution)/shard_map/while/body/eval_jaxpr/ppermute | solution.py:76
  611.3 22.7 %collective-permute-start.4 = (f32[4,128,1,256]{3,1,0,2:T(8,128)}, f32[4,128,1,256]{3,1,0,2:T(8,128)S(1)}, u32[]{:S(2)}, u32[]{:S(2)}) collective-permute-start(f32[4,128,1,256]{3,1,0,2:T(8,128)} %get-tuple-element.662), channel_id=1, source_target_pairs={{0,1},{1,2},{2,3},{3,4},{4,5},{5,6},{6,7},{7,8},{8,9},{9,10},{10,1... | collective-permute-start | bytes 1572872 | tf_op jit(solution)/shard_map/while/body/eval_jaxpr/ppermute | solution.py:75
  644.8 22.7 %collective-permute-start.5 = (f32[4,128,1,256]{3,1,0,2:T(8,128)}, f32[4,128,1,256]{3,1,0,2:T(8,128)S(1)}, u32[]{:S(2)}, u32[]{:S(2)}) collective-permute-start(f32[4,128,1,256]{3,1,0,2:T(8,128)} %get-tuple-element.663), channel_id=1, source_target_pairs={{0,1},{1,2},{2,3},{3,4},{4,5},{5,6},{6,7},{7,8},{8,9},{9,10},{10,1... | collective-permute-start | bytes 1572872 | tf_op jit(solution)/shard_map/while/body/eval_jaxpr/ppermute | solution.py:76
  644.8 22.7 %collective-permute-start.4 = (f32[4,128,1,256]{3,1,0,2:T(8,128)}, f32[4,128,1,256]{3,1,0,2:T(8,128)S(1)}, u32[]{:S(2)}, u32[]{:S(2)}) collective-permute-start(f32[4,128,1,256]{3,1,0,2:T(8,128)} %get-tuple-element.662), channel_id=1, source_target_pairs={{0,1},{1,2},{2,3},{3,4},{4,5},{5,6},{6,7},{7,8},{8,9},{9,10},{10,1... | collective-permute-start | bytes 1572872 | tf_op jit(solution)/shard_map/while/body/eval_jaxpr/ppermute | solution.py:75
  678.2 22.7 %collective-permute-start.5 = (f32[4,128,1,256]{3,1,0,2:T(8,128)}, f32[4,128,1,256]{3,1,0,2:T(8,128)S(1)}, u32[]{:S(2)}, u32[]{:S(2)}) collective-permute-start(f32[4,128,1,256]{3,1,0,2:T(8,128)} %get-tuple-element.663), channel_id=1, source_target_pairs={{0,1},{1,2},{2,3},{3,4},{4,5},{5,6},{6,7},{7,8},{8,9},{9,10},{10,1... | collective-permute-start | bytes 1572872 | tf_op jit(solution)/shard_map/while/body/eval_jaxpr/ppermute | solution.py:76
  678.3 22.7 %collective-permute-start.4 = (f32[4,128,1,256]{3,1,0,2:T(8,128)}, f32[4,128,1,256]{3,1,0,2:T(8,128)S(1)}, u32[]{:S(2)}, u32[]{:S(2)}) collective-permute-start(f32[4,128,1,256]{3,1,0,2:T(8,128)} %get-tuple-element.662), channel_id=1, source_target_pairs={{0,1},{1,2},{2,3},{3,4},{4,5},{5,6},{6,7},{7,8},{8,9},{9,10},{10,1... | collective-permute-start | bytes 1572872 | tf_op jit(solution)/shard_map/while/body/eval_jaxpr/ppermute | solution.py:75
  711.7 22.7 %collective-permute-start.5 = (f32[4,128,1,256]{3,1,0,2:T(8,128)}, f32[4,128,1,256]{3,1,0,2:T(8,128)S(1)}, u32[]{:S(2)}, u32[]{:S(2)}) collective-permute-start(f32[4,128,1,256]{3,1,0,2:T(8,128)} %get-tuple-element.663), channel_id=1, source_target_pairs={{0,1},{1,2},{2,3},{3,4},{4,5},{5,6},{6,7},{7,8},{8,9},{9,10},{10,1... | collective-permute-start | bytes 1572872 | tf_op jit(solution)/shard_map/while/body/eval_jaxpr/ppermute | solution.py:76
  711.8 22.7 %collective-permute-start.4 = (f32[4,128,1,256]{3,1,0,2:T(8,128)}, f32[4,128,1,256]{3,1,0,2:T(8,128)S(1)}, u32[]{:S(2)}, u32[]{:S(2)}) collective-permute-start(f32[4,128,1,256]{3,1,0,2:T(8,128)} %get-tuple-element.662), channel_id=1, source_target_pairs={{0,1},{1,2},{2,3},{3,4},{4,5},{5,6},{6,7},{7,8},{8,9},{9,10},{10,1... | collective-permute-start | bytes 1572872 | tf_op jit(solution)/shard_map/while/body/eval_jaxpr/ppermute | solution.py:75
  711.8 21.9 %collective-permute-start.2 = (bf16[4,128,1,256]{3,1,0,2:T(8,128)(2,1)}, bf16[4,128,1,256]{3,1,0,2:T(8,128)(2,1)S(1)}, u32[]{:S(2)}, u32[]{:S(2)}) collective-permute-start(bf16[4,128,1,256]{3,1,0,2:T(8,128)(2,1)} %get-tuple-element.660), channel_id=1, source_target_pairs={{0,1},{1,2},{2,3},{3,4},{4,5},{5,6},{6,7},{7,8},{8,9},{9,10},{10,1... | collective-permute-start | bytes 786440 | tf_op jit(solution)/shard_map/while/body/eval_jaxpr/ppermute | solution.py:73
  745.2 22.7 %collective-permute-start.5 = (f32[4,128,1,256]{3,1,0,2:T(8,128)}, f32[4,128,1,256]{3,1,0,2:T(8,128)S(1)}, u32[]{:S(2)}, u32[]{:S(2)}) collective-permute-start(f32[4,128,1,256]{3,1,0,2:T(8,128)} %get-tuple-element.663), channel_id=1, source_target_pairs={{0,1},{1,2},{2,3},{3,4},{4,5},{5,6},{6,7},{7,8},{8,9},{9,10},{10,1... | collective-permute-start | bytes 1572872 | tf_op jit(solution)/shard_map/while/body/eval_jaxpr/ppermute | solution.py:76
  745.3 22.7 %collective-permute-start.4 = (f32[4,128,1,256]{3,1,0,2:T(8,128)}, f32[4,128,1,256]{3,1,0,2:T(8,128)S(1)}, u32[]{:S(2)}, u32[]{:S(2)}) collective-permute-start(f32[4,128,1,256]{3,1,0,2:T(8,128)} %get-tuple-element.662), channel_id=1, source_target_pairs={{0,1},{1,2},{2,3},{3,4},{4,5},{5,6},{6,7},{7,8},{8,9},{9,10},{10,1... | collective-permute-start | bytes 1572872 | tf_op jit(solution)/shard_map/while/body/eval_jaxpr/ppermute | solution.py:75
  778.7 22.7 %collective-permute-start.5 = (f32[4,128,1,256]{3,1,0,2:T(8,128)}, f32[4,128,1,256]{3,1,0,2:T(8,128)S(1)}, u32[]{:S(2)}, u32[]{:S(2)}) collective-permute-start(f32[4,128,1,256]{3,1,0,2:T(8,128)} %get-tuple-element.663), channel_id=1, source_target_pairs={{0,1},{1,2},{2,3},{3,4},{4,5},{5,6},{6,7},{7,8},{8,9},{9,10},{10,1... | collective-permute-start | bytes 1572872 | tf_op jit(solution)/shard_map/while/body/eval_jaxpr/ppermute | solution.py:76
  778.8 22.7 %collective-permute-start.4 = (f32[4,128,1,256]{3,1,0,2:T(8,128)}, f32[4,128,1,256]{3,1,0,2:T(8,128)S(1)}, u32[]{:S(2)}, u32[]{:S(2)}) collective-permute-start(f32[4,128,1,256]{3,1,0,2:T(8,128)} %get-tuple-element.662), channel_id=1, source_target_pairs={{0,1},{1,2},{2,3},{3,4},{4,5},{5,6},{6,7},{7,8},{8,9},{9,10},{10,1... | collective-permute-start | bytes 1572872 | tf_op jit(solution)/shard_map/while/body/eval_jaxpr/ppermute | solution.py:75
  812.2 22.7 %collective-permute-start.5 = (f32[4,128,1,256]{3,1,0,2:T(8,128)}, f32[4,128,1,256]{3,1,0,2:T(8,128)S(1)}, u32[]{:S(2)}, u32[]{:S(2)}) collective-permute-start(f32[4,128,1,256]{3,1,0,2:T(8,128)} %get-tuple-element.663), channel_id=1, source_target_pairs={{0,1},{1,2},{2,3},{3,4},{4,5},{5,6},{6,7},{7,8},{8,9},{9,10},{10,1... | collective-permute-start | bytes 1572872 | tf_op jit(solution)/shard_map/while/body/eval_jaxpr/ppermute | solution.py:76
  812.2 22.7 %collective-permute-start.4 = (f32[4,128,1,256]{3,1,0,2:T(8,128)}, f32[4,128,1,256]{3,1,0,2:T(8,128)S(1)}, u32[]{:S(2)}, u32[]{:S(2)}) collective-permute-start(f32[4,128,1,256]{3,1,0,2:T(8,128)} %get-tuple-element.662), channel_id=1, source_target_pairs={{0,1},{1,2},{2,3},{3,4},{4,5},{5,6},{6,7},{7,8},{8,9},{9,10},{10,1... | collective-permute-start | bytes 1572872 | tf_op jit(solution)/shard_map/while/body/eval_jaxpr/ppermute | solution.py:75
  812.3 21.9 %collective-permute-start.2 = (bf16[4,128,1,256]{3,1,0,2:T(8,128)(2,1)}, bf16[4,128,1,256]{3,1,0,2:T(8,128)(2,1)S(1)}, u32[]{:S(2)}, u32[]{:S(2)}) collective-permute-start(bf16[4,128,1,256]{3,1,0,2:T(8,128)(2,1)} %get-tuple-element.660), channel_id=1, source_target_pairs={{0,1},{1,2},{2,3},{3,4},{4,5},{5,6},{6,7},{7,8},{8,9},{9,10},{10,1... | collective-permute-start | bytes 786440 | tf_op jit(solution)/shard_map/while/body/eval_jaxpr/ppermute | solution.py:73
  845.7 22.7 %collective-permute-start.5 = (f32[4,128,1,256]{3,1,0,2:T(8,128)}, f32[4,128,1,256]{3,1,0,2:T(8,128)S(1)}, u32[]{:S(2)}, u32[]{:S(2)}) collective-permute-start(f32[4,128,1,256]{3,1,0,2:T(8,128)} %get-tuple-element.663), channel_id=1, source_target_pairs={{0,1},{1,2},{2,3},{3,4},{4,5},{5,6},{6,7},{7,8},{8,9},{9,10},{10,1... | collective-permute-start | bytes 1572872 | tf_op jit(solution)/shard_map/while/body/eval_jaxpr/ppermute | solution.py:76
  845.7 22.7 %collective-permute-start.4 = (f32[4,128,1,256]{3,1,0,2:T(8,128)}, f32[4,128,1,256]{3,1,0,2:T(8,128)S(1)}, u32[]{:S(2)}, u32[]{:S(2)}) collective-permute-start(f32[4,128,1,256]{3,1,0,2:T(8,128)} %get-tuple-element.662), channel_id=1, source_target_pairs={{0,1},{1,2},{2,3},{3,4},{4,5},{5,6},{6,7},{7,8},{8,9},{9,10},{10,1... | collective-permute-start | bytes 1572872 | tf_op jit(solution)/shard_map/while/body/eval_jaxpr/ppermute | solution.py:75
  879.2 22.7 %collective-permute-start.5 = (f32[4,128,1,256]{3,1,0,2:T(8,128)}, f32[4,128,1,256]{3,1,0,2:T(8,128)S(1)}, u32[]{:S(2)}, u32[]{:S(2)}) collective-permute-start(f32[4,128,1,256]{3,1,0,2:T(8,128)} %get-tuple-element.663), channel_id=1, source_target_pairs={{0,1},{1,2},{2,3},{3,4},{4,5},{5,6},{6,7},{7,8},{8,9},{9,10},{10,1... | collective-permute-start | bytes 1572872 | tf_op jit(solution)/shard_map/while/body/eval_jaxpr/ppermute | solution.py:76
  879.2 22.7 %collective-permute-start.4 = (f32[4,128,1,256]{3,1,0,2:T(8,128)}, f32[4,128,1,256]{3,1,0,2:T(8,128)S(1)}, u32[]{:S(2)}, u32[]{:S(2)}) collective-permute-start(f32[4,128,1,256]{3,1,0,2:T(8,128)} %get-tuple-element.662), channel_id=1, source_target_pairs={{0,1},{1,2},{2,3},{3,4},{4,5},{5,6},{6,7},{7,8},{8,9},{9,10},{10,1... | collective-permute-start | bytes 1572872 | tf_op jit(solution)/shard_map/while/body/eval_jaxpr/ppermute | solution.py:75
  912.7 22.7 %collective-permute-start.5 = (f32[4,128,1,256]{3,1,0,2:T(8,128)}, f32[4,128,1,256]{3,1,0,2:T(8,128)S(1)}, u32[]{:S(2)}, u32[]{:S(2)}) collective-permute-start(f32[4,128,1,256]{3,1,0,2:T(8,128)} %get-tuple-element.663), channel_id=1, source_target_pairs={{0,1},{1,2},{2,3},{3,4},{4,5},{5,6},{6,7},{7,8},{8,9},{9,10},{10,1... | collective-permute-start | bytes 1572872 | tf_op jit(solution)/shard_map/while/body/eval_jaxpr/ppermute | solution.py:76
  912.7 22.7 %collective-permute-start.4 = (f32[4,128,1,256]{3,1,0,2:T(8,128)}, f32[4,128,1,256]{3,1,0,2:T(8,128)S(1)}, u32[]{:S(2)}, u32[]{:S(2)}) collective-permute-start(f32[4,128,1,256]{3,1,0,2:T(8,128)} %get-tuple-element.662), channel_id=1, source_target_pairs={{0,1},{1,2},{2,3},{3,4},{4,5},{5,6},{6,7},{7,8},{8,9},{9,10},{10,1... | collective-permute-start | bytes 1572872 | tf_op jit(solution)/shard_map/while/body/eval_jaxpr/ppermute | solution.py:75
  946.2 22.7 %collective-permute-start.5 = (f32[4,128,1,256]{3,1,0,2:T(8,128)}, f32[4,128,1,256]{3,1,0,2:T(8,128)S(1)}, u32[]{:S(2)}, u32[]{:S(2)}) collective-permute-start(f32[4,128,1,256]{3,1,0,2:T(8,128)} %get-tuple-element.663), channel_id=1, source_target_pairs={{0,1},{1,2},{2,3},{3,4},{4,5},{5,6},{6,7},{7,8},{8,9},{9,10},{10,1... | collective-permute-start | bytes 1572872 | tf_op jit(solution)/shard_map/while/body/eval_jaxpr/ppermute | solution.py:76
  946.2 22.7 %collective-permute-start.4 = (f32[4,128,1,256]{3,1,0,2:T(8,128)}, f32[4,128,1,256]{3,1,0,2:T(8,128)S(1)}, u32[]{:S(2)}, u32[]{:S(2)}) collective-permute-start(f32[4,128,1,256]{3,1,0,2:T(8,128)} %get-tuple-element.662), channel_id=1, source_target_pairs={{0,1},{1,2},{2,3},{3,4},{4,5},{5,6},{6,7},{7,8},{8,9},{9,10},{10,1... | collective-permute-start | bytes 1572872 | tf_op jit(solution)/shard_map/while/body/eval_jaxpr/ppermute | solution.py:75
  979.7 22.7 %collective-permute-start.5 = (f32[4,128,1,256]{3,1,0,2:T(8,128)}, f32[4,128,1,256]{3,1,0,2:T(8,128)S(1)}, u32[]{:S(2)}, u32[]{:S(2)}) collective-permute-start(f32[4,128,1,256]{3,1,0,2:T(8,128)} %get-tuple-element.663), channel_id=1, source_target_pairs={{0,1},{1,2},{2,3},{3,4},{4,5},{5,6},{6,7},{7,8},{8,9},{9,10},{10,1... | collective-permute-start | bytes 1572872 | tf_op jit(solution)/shard_map/while/body/eval_jaxpr/ppermute | solution.py:76
  979.7 22.7 %collective-permute-start.4 = (f32[4,128,1,256]{3,1,0,2:T(8,128)}, f32[4,128,1,256]{3,1,0,2:T(8,128)S(1)}, u32[]{:S(2)}, u32[]{:S(2)}) collective-permute-start(f32[4,128,1,256]{3,1,0,2:T(8,128)} %get-tuple-element.662), channel_id=1, source_target_pairs={{0,1},{1,2},{2,3},{3,4},{4,5},{5,6},{6,7},{7,8},{8,9},{9,10},{10,1... | collective-permute-start | bytes 1572872 | tf_op jit(solution)/shard_map/while/body/eval_jaxpr/ppermute | solution.py:75
  1013.2 22.7 %collective-permute-start.5 = (f32[4,128,1,256]{3,1,0,2:T(8,128)}, f32[4,128,1,256]{3,1,0,2:T(8,128)S(1)}, u32[]{:S(2)}, u32[]{:S(2)}) collective-permute-start(f32[4,128,1,256]{3,1,0,2:T(8,128)} %get-tuple-element.663), channel_id=1, source_target_pairs={{0,1},{1,2},{2,3},{3,4},{4,5},{5,6},{6,7},{7,8},{8,9},{9,10},{10,1... | collective-permute-start | bytes 1572872 | tf_op jit(solution)/shard_map/while/body/eval_jaxpr/ppermute | solution.py:76
  1013.2 22.7 %collective-permute-start.4 = (f32[4,128,1,256]{3,1,0,2:T(8,128)}, f32[4,128,1,256]{3,1,0,2:T(8,128)S(1)}, u32[]{:S(2)}, u32[]{:S(2)}) collective-permute-start(f32[4,128,1,256]{3,1,0,2:T(8,128)} %get-tuple-element.662), channel_id=1, source_target_pairs={{0,1},{1,2},{2,3},{3,4},{4,5},{5,6},{6,7},{7,8},{8,9},{9,10},{10,1... | collective-permute-start | bytes 1572872 | tf_op jit(solution)/shard_map/while/body/eval_jaxpr/ppermute | solution.py:75
  1046.7 22.7 %collective-permute-start.5 = (f32[4,128,1,256]{3,1,0,2:T(8,128)}, f32[4,128,1,256]{3,1,0,2:T(8,128)S(1)}, u32[]{:S(2)}, u32[]{:S(2)}) collective-permute-start(f32[4,128,1,256]{3,1,0,2:T(8,128)} %get-tuple-element.663), channel_id=1, source_target_pairs={{0,1},{1,2},{2,3},{3,4},{4,5},{5,6},{6,7},{7,8},{8,9},{9,10},{10,1... | collective-permute-start | bytes 1572872 | tf_op jit(solution)/shard_map/while/body/eval_jaxpr/ppermute | solution.py:76
  1046.7 22.7 %collective-permute-start.4 = (f32[4,128,1,256]{3,1,0,2:T(8,128)}, f32[4,128,1,256]{3,1,0,2:T(8,128)S(1)}, u32[]{:S(2)}, u32[]{:S(2)}) collective-permute-start(f32[4,128,1,256]{3,1,0,2:T(8,128)} %get-tuple-element.662), channel_id=1, source_target_pairs={{0,1},{1,2},{2,3},{3,4},{4,5},{5,6},{6,7},{7,8},{8,9},{9,10},{10,1... | collective-permute-start | bytes 1572872 | tf_op jit(solution)/shard_map/while/body/eval_jaxpr/ppermute | solution.py:75
  1080.2 22.7 %collective-permute-start.5 = (f32[4,128,1,256]{3,1,0,2:T(8,128)}, f32[4,128,1,256]{3,1,0,2:T(8,128)S(1)}, u32[]{:S(2)}, u32[]{:S(2)}) collective-permute-start(f32[4,128,1,256]{3,1,0,2:T(8,128)} %get-tuple-element.663), channel_id=1, source_target_pairs={{0,1},{1,2},{2,3},{3,4},{4,5},{5,6},{6,7},{7,8},{8,9},{9,10},{10,1... | collective-permute-start | bytes 1572872 | tf_op jit(solution)/shard_map/while/body/eval_jaxpr/ppermute | solution.py:76
  1080.2 22.7 %collective-permute-start.4 = (f32[4,128,1,256]{3,1,0,2:T(8,128)}, f32[4,128,1,256]{3,1,0,2:T(8,128)S(1)}, u32[]{:S(2)}, u32[]{:S(2)}) collective-permute-start(f32[4,128,1,256]{3,1,0,2:T(8,128)} %get-tuple-element.662), channel_id=1, source_target_pairs={{0,1},{1,2},{2,3},{3,4},{4,5},{5,6},{6,7},{7,8},{8,9},{9,10},{10,1... | collective-permute-start | bytes 1572872 | tf_op jit(solution)/shard_map/while/body/eval_jaxpr/ppermute | solution.py:75
  1113.7 22.7 %collective-permute-start.5 = (f32[4,128,1,256]{3,1,0,2:T(8,128)}, f32[4,128,1,256]{3,1,0,2:T(8,128)S(1)}, u32[]{:S(2)}, u32[]{:S(2)}) collective-permute-start(f32[4,128,1,256]{3,1,0,2:T(8,128)} %get-tuple-element.663), channel_id=1, source_target_pairs={{0,1},{1,2},{2,3},{3,4},{4,5},{5,6},{6,7},{7,8},{8,9},{9,10},{10,1... | collective-permute-start | bytes 1572872 | tf_op jit(solution)/shard_map/while/body/eval_jaxpr/ppermute | solution.py:76
  1113.7 22.7 %collective-permute-start.4 = (f32[4,128,1,256]{3,1,0,2:T(8,128)}, f32[4,128,1,256]{3,1,0,2:T(8,128)S(1)}, u32[]{:S(2)}, u32[]{:S(2)}) collective-permute-start(f32[4,128,1,256]{3,1,0,2:T(8,128)} %get-tuple-element.662), channel_id=1, source_target_pairs={{0,1},{1,2},{2,3},{3,4},{4,5},{5,6},{6,7},{7,8},{8,9},{9,10},{10,1... | collective-permute-start | bytes 1572872 | tf_op jit(solution)/shard_map/while/body/eval_jaxpr/ppermute | solution.py:75
  1147.2 22.7 %collective-permute-start.5 = (f32[4,128,1,256]{3,1,0,2:T(8,128)}, f32[4,128,1,256]{3,1,0,2:T(8,128)S(1)}, u32[]{:S(2)}, u32[]{:S(2)}) collective-permute-start(f32[4,128,1,256]{3,1,0,2:T(8,128)} %get-tuple-element.663), channel_id=1, source_target_pairs={{0,1},{1,2},{2,3},{3,4},{4,5},{5,6},{6,7},{7,8},{8,9},{9,10},{10,1... | collective-permute-start | bytes 1572872 | tf_op jit(solution)/shard_map/while/body/eval_jaxpr/ppermute | solution.py:76
  1147.2 22.7 %collective-permute-start.4 = (f32[4,128,1,256]{3,1,0,2:T(8,128)}, f32[4,128,1,256]{3,1,0,2:T(8,128)S(1)}, u32[]{:S(2)}, u32[]{:S(2)}) collective-permute-start(f32[4,128,1,256]{3,1,0,2:T(8,128)} %get-tuple-element.662), channel_id=1, source_target_pairs={{0,1},{1,2},{2,3},{3,4},{4,5},{5,6},{6,7},{7,8},{8,9},{9,10},{10,1... | collective-permute-start | bytes 1572872 | tf_op jit(solution)/shard_map/while/body/eval_jaxpr/ppermute | solution.py:75
  1180.7 22.7 %collective-permute-start.5 = (f32[4,128,1,256]{3,1,0,2:T(8,128)}, f32[4,128,1,256]{3,1,0,2:T(8,128)S(1)}, u32[]{:S(2)}, u32[]{:S(2)}) collective-permute-start(f32[4,128,1,256]{3,1,0,2:T(8,128)} %get-tuple-element.663), channel_id=1, source_target_pairs={{0,1},{1,2},{2,3},{3,4},{4,5},{5,6},{6,7},{7,8},{8,9},{9,10},{10,1... | collective-permute-start | bytes 1572872 | tf_op jit(solution)/shard_map/while/body/eval_jaxpr/ppermute | solution.py:76
  1180.7 22.7 %collective-permute-start.4 = (f32[4,128,1,256]{3,1,0,2:T(8,128)}, f32[4,128,1,256]{3,1,0,2:T(8,128)S(1)}, u32[]{:S(2)}, u32[]{:S(2)}) collective-permute-start(f32[4,128,1,256]{3,1,0,2:T(8,128)} %get-tuple-element.662), channel_id=1, source_target_pairs={{0,1},{1,2},{2,3},{3,4},{4,5},{5,6},{6,7},{7,8},{8,9},{9,10},{10,1... | collective-permute-start | bytes 1572872 | tf_op jit(solution)/shard_map/while/body/eval_jaxpr/ppermute | solution.py:75
  1214.2 22.7 %collective-permute-start.5 = (f32[4,128,1,256]{3,1,0,2:T(8,128)}, f32[4,128,1,256]{3,1,0,2:T(8,128)S(1)}, u32[]{:S(2)}, u32[]{:S(2)}) collective-permute-start(f32[4,128,1,256]{3,1,0,2:T(8,128)} %get-tuple-element.663), channel_id=1, source_target_pairs={{0,1},{1,2},{2,3},{3,4},{4,5},{5,6},{6,7},{7,8},{8,9},{9,10},{10,1... | collective-permute-start | bytes 1572872 | tf_op jit(solution)/shard_map/while/body/eval_jaxpr/ppermute | solution.py:76
  1214.2 22.7 %collective-permute-start.4 = (f32[4,128,1,256]{3,1,0,2:T(8,128)}, f32[4,128,1,256]{3,1,0,2:T(8,128)S(1)}, u32[]{:S(2)}, u32[]{:S(2)}) collective-permute-start(f32[4,128,1,256]{3,1,0,2:T(8,128)} %get-tuple-element.662), channel_id=1, source_target_pairs={{0,1},{1,2},{2,3},{3,4},{4,5},{5,6},{6,7},{7,8},{8,9},{9,10},{10,1... | collective-permute-start | bytes 1572872 | tf_op jit(solution)/shard_map/while/body/eval_jaxpr/ppermute | solution.py:75
  1247.7 22.7 %collective-permute-start.5 = (f32[4,128,1,256]{3,1,0,2:T(8,128)}, f32[4,128,1,256]{3,1,0,2:T(8,128)S(1)}, u32[]{:S(2)}, u32[]{:S(2)}) collective-permute-start(f32[4,128,1,256]{3,1,0,2:T(8,128)} %get-tuple-element.663), channel_id=1, source_target_pairs={{0,1},{1,2},{2,3},{3,4},{4,5},{5,6},{6,7},{7,8},{8,9},{9,10},{10,1... | collective-permute-start | bytes 1572872 | tf_op jit(solution)/shard_map/while/body/eval_jaxpr/ppermute | solution.py:76
  1247.7 22.7 %collective-permute-start.4 = (f32[4,128,1,256]{3,1,0,2:T(8,128)}, f32[4,128,1,256]{3,1,0,2:T(8,128)S(1)}, u32[]{:S(2)}, u32[]{:S(2)}) collective-permute-start(f32[4,128,1,256]{3,1,0,2:T(8,128)} %get-tuple-element.662), channel_id=1, source_target_pairs={{0,1},{1,2},{2,3},{3,4},{4,5},{5,6},{6,7},{7,8},{8,9},{9,10},{10,1... | collective-permute-start | bytes 1572872 | tf_op jit(solution)/shard_map/while/body/eval_jaxpr/ppermute | solution.py:75
  1281.2 22.7 %collective-permute-start.5 = (f32[4,128,1,256]{3,1,0,2:T(8,128)}, f32[4,128,1,256]{3,1,0,2:T(8,128)S(1)}, u32[]{:S(2)}, u32[]{:S(2)}) collective-permute-start(f32[4,128,1,256]{3,1,0,2:T(8,128)} %get-tuple-element.663), channel_id=1, source_target_pairs={{0,1},{1,2},{2,3},{3,4},{4,5},{5,6},{6,7},{7,8},{8,9},{9,10},{10,1... | collective-permute-start | bytes 1572872 | tf_op jit(solution)/shard_map/while/body/eval_jaxpr/ppermute | solution.py:76
  1281.2 22.7 %collective-permute-start.4 = (f32[4,128,1,256]{3,1,0,2:T(8,128)}, f32[4,128,1,256]{3,1,0,2:T(8,128)S(1)}, u32[]{:S(2)}, u32[]{:S(2)}) collective-permute-start(f32[4,128,1,256]{3,1,0,2:T(8,128)} %get-tuple-element.662), channel_id=1, source_target_pairs={{0,1},{1,2},{2,3},{3,4},{4,5},{5,6},{6,7},{7,8},{8,9},{9,10},{10,1... | collective-permute-start | bytes 1572872 | tf_op jit(solution)/shard_map/while/body/eval_jaxpr/ppermute | solution.py:75
  1314.7 22.7 %collective-permute-start.5 = (f32[4,128,1,256]{3,1,0,2:T(8,128)}, f32[4,128,1,256]{3,1,0,2:T(8,128)S(1)}, u32[]{:S(2)}, u32[]{:S(2)}) collective-permute-start(f32[4,128,1,256]{3,1,0,2:T(8,128)} %get-tuple-element.663), channel_id=1, source_target_pairs={{0,1},{1,2},{2,3},{3,4},{4,5},{5,6},{6,7},{7,8},{8,9},{9,10},{10,1... | collective-permute-start | bytes 1572872 | tf_op jit(solution)/shard_map/while/body/eval_jaxpr/ppermute | solution.py:76
  1314.7 22.7 %collective-permute-start.4 = (f32[4,128,1,256]{3,1,0,2:T(8,128)}, f32[4,128,1,256]{3,1,0,2:T(8,128)S(1)}, u32[]{:S(2)}, u32[]{:S(2)}) collective-permute-start(f32[4,128,1,256]{3,1,0,2:T(8,128)} %get-tuple-element.662), channel_id=1, source_target_pairs={{0,1},{1,2},{2,3},{3,4},{4,5},{5,6},{6,7},{7,8},{8,9},{9,10},{10,1... | collective-permute-start | bytes 1572872 | tf_op jit(solution)/shard_map/while/body/eval_jaxpr/ppermute | solution.py:75
  1339.0 22.7 %collective-permute-start.5 = (f32[4,128,1,256]{3,1,0,2:T(8,128)}, f32[4,128,1,256]{3,1,0,2:T(8,128)S(1)}, u32[]{:S(2)}, u32[]{:S(2)}) collective-permute-start(f32[4,128,1,256]{3,1,0,2:T(8,128)} %get-tuple-element.663), channel_id=1, source_target_pairs={{0,1},{1,2},{2,3},{3,4},{4,5},{5,6},{6,7},{7,8},{8,9},{9,10},{10,1... | collective-permute-start | bytes 1572872 | tf_op jit(solution)/shard_map/while/body/eval_jaxpr/ppermute | solution.py:76
  1339.0 22.7 %collective-permute-start.4 = (f32[4,128,1,256]{3,1,0,2:T(8,128)}, f32[4,128,1,256]{3,1,0,2:T(8,128)S(1)}, u32[]{:S(2)}, u32[]{:S(2)}) collective-permute-start(f32[4,128,1,256]{3,1,0,2:T(8,128)} %get-tuple-element.662), channel_id=1, source_target_pairs={{0,1},{1,2},{2,3},{3,4},{4,5},{5,6},{6,7},{7,8},{8,9},{9,10},{10,1... | collective-permute-start | bytes 1572872 | tf_op jit(solution)/shard_map/while/body/eval_jaxpr/ppermute | solution.py:75
  1363.3 22.7 %collective-permute-start.5 = (f32[4,128,1,256]{3,1,0,2:T(8,128)}, f32[4,128,1,256]{3,1,0,2:T(8,128)S(1)}, u32[]{:S(2)}, u32[]{:S(2)}) collective-permute-start(f32[4,128,1,256]{3,1,0,2:T(8,128)} %get-tuple-element.663), channel_id=1, source_target_pairs={{0,1},{1,2},{2,3},{3,4},{4,5},{5,6},{6,7},{7,8},{8,9},{9,10},{10,1... | collective-permute-start | bytes 1572872 | tf_op jit(solution)/shard_map/while/body/eval_jaxpr/ppermute | solution.py:76
  1363.3 22.7 %collective-permute-start.4 = (f32[4,128,1,256]{3,1,0,2:T(8,128)}, f32[4,128,1,256]{3,1,0,2:T(8,128)S(1)}, u32[]{:S(2)}, u32[]{:S(2)}) collective-permute-start(f32[4,128,1,256]{3,1,0,2:T(8,128)} %get-tuple-element.662), channel_id=1, source_target_pairs={{0,1},{1,2},{2,3},{3,4},{4,5},{5,6},{6,7},{7,8},{8,9},{9,10},{10,1... | collective-permute-start | bytes 1572872 | tf_op jit(solution)/shard_map/while/body/eval_jaxpr/ppermute | solution.py:75
  1387.5 22.7 %collective-permute-start.5 = (f32[4,128,1,256]{3,1,0,2:T(8,128)}, f32[4,128,1,256]{3,1,0,2:T(8,128)S(1)}, u32[]{:S(2)}, u32[]{:S(2)}) collective-permute-start(f32[4,128,1,256]{3,1,0,2:T(8,128)} %get-tuple-element.663), channel_id=1, source_target_pairs={{0,1},{1,2},{2,3},{3,4},{4,5},{5,6},{6,7},{7,8},{8,9},{9,10},{10,1... | collective-permute-start | bytes 1572872 | tf_op jit(solution)/shard_map/while/body/eval_jaxpr/ppermute | solution.py:76
  1387.5 22.7 %collective-permute-start.4 = (f32[4,128,1,256]{3,1,0,2:T(8,128)}, f32[4,128,1,256]{3,1,0,2:T(8,128)S(1)}, u32[]{:S(2)}, u32[]{:S(2)}) collective-permute-start(f32[4,128,1,256]{3,1,0,2:T(8,128)} %get-tuple-element.662), channel_id=1, source_target_pairs={{0,1},{1,2},{2,3},{3,4},{4,5},{5,6},{6,7},{7,8},{8,9},{9,10},{10,1... | collective-permute-start | bytes 1572872 | tf_op jit(solution)/shard_map/while/body/eval_jaxpr/ppermute | solution.py:75
  1411.8 22.7 %collective-permute-start.5 = (f32[4,128,1,256]{3,1,0,2:T(8,128)}, f32[4,128,1,256]{3,1,0,2:T(8,128)S(1)}, u32[]{:S(2)}, u32[]{:S(2)}) collective-permute-start(f32[4,128,1,256]{3,1,0,2:T(8,128)} %get-tuple-element.663), channel_id=1, source_target_pairs={{0,1},{1,2},{2,3},{3,4},{4,5},{5,6},{6,7},{7,8},{8,9},{9,10},{10,1... | collective-permute-start | bytes 1572872 | tf_op jit(solution)/shard_map/while/body/eval_jaxpr/ppermute | solution.py:76
  1411.8 22.7 %collective-permute-start.4 = (f32[4,128,1,256]{3,1,0,2:T(8,128)}, f32[4,128,1,256]{3,1,0,2:T(8,128)S(1)}, u32[]{:S(2)}, u32[]{:S(2)}) collective-permute-start(f32[4,128,1,256]{3,1,0,2:T(8,128)} %get-tuple-element.662), channel_id=1, source_target_pairs={{0,1},{1,2},{2,3},{3,4},{4,5},{5,6},{6,7},{7,8},{8,9},{9,10},{10,1... | collective-permute-start | bytes 1572872 | tf_op jit(solution)/shard_map/while/body/eval_jaxpr/ppermute | solution.py:75
  1436.1 22.7 %collective-permute-start.5 = (f32[4,128,1,256]{3,1,0,2:T(8,128)}, f32[4,128,1,256]{3,1,0,2:T(8,128)S(1)}, u32[]{:S(2)}, u32[]{:S(2)}) collective-permute-start(f32[4,128,1,256]{3,1,0,2:T(8,128)} %get-tuple-element.663), channel_id=1, source_target_pairs={{0,1},{1,2},{2,3},{3,4},{4,5},{5,6},{6,7},{7,8},{8,9},{9,10},{10,1... | collective-permute-start | bytes 1572872 | tf_op jit(solution)/shard_map/while/body/eval_jaxpr/ppermute | solution.py:76
  1436.1 22.7 %collective-permute-start.4 = (f32[4,128,1,256]{3,1,0,2:T(8,128)}, f32[4,128,1,256]{3,1,0,2:T(8,128)S(1)}, u32[]{:S(2)}, u32[]{:S(2)}) collective-permute-start(f32[4,128,1,256]{3,1,0,2:T(8,128)} %get-tuple-element.662), channel_id=1, source_target_pairs={{0,1},{1,2},{2,3},{3,4},{4,5},{5,6},{6,7},{7,8},{8,9},{9,10},{10,1... | collective-permute-start | bytes 1572872 | tf_op jit(solution)/shard_map/while/body/eval_jaxpr/ppermute | solution.py:75
  1460.3 22.7 %collective-permute-start.5 = (f32[4,128,1,256]{3,1,0,2:T(8,128)}, f32[4,128,1,256]{3,1,0,2:T(8,128)S(1)}, u32[]{:S(2)}, u32[]{:S(2)}) collective-permute-start(f32[4,128,1,256]{3,1,0,2:T(8,128)} %get-tuple-element.663), channel_id=1, source_target_pairs={{0,1},{1,2},{2,3},{3,4},{4,5},{5,6},{6,7},{7,8},{8,9},{9,10},{10,1... | collective-permute-start | bytes 1572872 | tf_op jit(solution)/shard_map/while/body/eval_jaxpr/ppermute | solution.py:76
  1460.3 22.7 %collective-permute-start.4 = (f32[4,128,1,256]{3,1,0,2:T(8,128)}, f32[4,128,1,256]{3,1,0,2:T(8,128)S(1)}, u32[]{:S(2)}, u32[]{:S(2)}) collective-permute-start(f32[4,128,1,256]{3,1,0,2:T(8,128)} %get-tuple-element.662), channel_id=1, source_target_pairs={{0,1},{1,2},{2,3},{3,4},{4,5},{5,6},{6,7},{7,8},{8,9},{9,10},{10,1... | collective-permute-start | bytes 1572872 | tf_op jit(solution)/shard_map/while/body/eval_jaxpr/ppermute | solution.py:75
  (251 other events, 2089.9 us)
where the time goes:
time: 1500 us
  waiting for transfers between devices  953 us (64%)
  local copies, waits for them, and re-layouts  314 us (21%)
  matrix products  193 us (13%)
  other arithmetic  19.1 us (1%)
    ppermute x31, waiting for transfers between devices, backward_body(): value_cur = lax.ppermute(value_cur, 'cp', shift_pairs)  589 us
    ppermute x31, waiting for transfers between devices, forward_body(): value_cur = lax.ppermute(value_cur, 'cp', shift_pairs)  238 us
    cond x264, local copies, waits for them, and re-layouts  174 us
    while x186, local copies, waits for them, and re-layouts  124 us
    ppermute x31, waiting for transfers between devices, forward_body(): key_cur = lax.ppermute(key_cur, 'cp', shift_pairs)  87.1 us
    dot_general x25, matrix products, backward_step(): jnp.einsum('bqgrd,bkgd->bgrqk', grad5, value_blk, preferred_element_type=...  45.6 us
    dot_general x25, matrix products, forward_step(): jnp.einsum('bgrqk,bkgd->bgrqd', weights.astype(jnp.bfloat16), value_blk,...  43.8 us
    dot_general x49, matrix products, block_scores(): jnp.einsum('bqgrd,bkgd->bgrqk', query5, key_blk, preferred_element_type=j...  41.9 us
  transfers between devices with their start and end apart: 188, of which 126 were waited for; matrix products, arithmetic and copies ran while one was open for 5% of the time, Pallas kernels for 0%

commit v1 on v0

v1 whole, which is shorter than its diff:
```python
import functools
import math

import jax
import jax.numpy as jnp
from jax import lax
from jax.experimental import pallas as pl
from jax.experimental.pallas import tpu as pltpu
from jax.sharding import PartitionSpec as P

F32 = jnp.float32
BF16 = jnp.bfloat16
LN2 = math.log(2.0)


def dot(lhs, rhs):
    return jnp.dot(lhs, rhs, preferred_element_type=F32)


def attention_kernel(q_in, do_in, k_in, v_in, out, lse_out, dq_out, dk_out, dv_out,
                     qs, dos, qt, dot_t, kv, ot, ot_low, o_st, m_s, l_s, lse2, delta, lse_st, p_s, ds_s,
                     dqt, dq_st, dkdv, sib, peer, fin,
                     loc_sem, kv1_s, kv1_r, kv2_s, kvd_s, kv_r, q_sem, do_sem, o_sem, ls_sem, dq_sem,
                     r1_s, r1_r, r2_s, r2_r, r3_s, r3_r):
    tokens, head_dim = k_in.shape[1], k_in.shape[2]
    rows = q_in.shape[1]
    heads = rows // tokens
    blocks = kv.shape[1]
    chunks = blocks // 2
    keys = 2 * tokens
    side = 4
    scale = head_dim ** -0.5
    alpha = scale / LN2
    tile = min(256, rows)

    me = lax.axis_index("cp")
    core = me % 2
    chip = me // 2
    x, y = chip % side, chip // side
    qx, qy = x // 2, y // 2
    ux, uy = x + qx * (3 - 2 * x), y + qy * (3 - 2 * y)
    batch = 2 * qy + qx
    sibling = me + 1 - 2 * core

    def flip(f):
        fx, fy = f % 2, f // 2
        return ((y + fy * (3 - 2 * y)) * side + x + fx * (3 - 2 * x)) * 2 + core

    def flip_batch(f):
        fx, fy = f % 2, f // 2
        return 2 * (qy + fy * (1 - 2 * qy)) + qx + fx * (1 - 2 * qx)

    def group(a):
        ax, ay = a % 2, a // 2
        return ((y + ay * (1 + 4 * qy - 2 * y)) * side + x + ax * (1 + 4 * qx - 2 * x)) * 2 + core

    def remote(src, dst, send, recv, device):
        return pltpu.make_async_remote_copy(
            src_ref=src, dst_ref=dst, send_sem=send, recv_sem=recv,
            device_id={"cp": device}, device_id_type=pl.DeviceIdType.MESH)

    barrier = pltpu.get_barrier_semaphore()
    for device in [flip(f) for f in (1, 2, 3)] + [group(a) for a in (1, 2, 3)] + [sibling]:
        pl.semaphore_signal(barrier, inc=1, device_id={"cp": device}, device_id_type=pl.DeviceIdType.MESH)
    pl.semaphore_wait(barrier, 7)

    own = [
        pltpu.make_async_copy(k_in.at[batch], kv.at[0, me], loc_sem.at[0]),
        pltpu.make_async_copy(v_in.at[batch], kv.at[1, me], loc_sem.at[1]),
        pltpu.make_async_copy(q_in.at[batch], qs.at[0], loc_sem.at[2]),
        pltpu.make_async_copy(do_in.at[batch], dos.at[0], loc_sem.at[3]),
    ]
    for copy in own:
        copy.start()

    def kv1(f, which):
        src = (k_in, v_in)[which]
        return remote(src.at[flip_batch(f)], kv.at[which, me], kv1_s.at[which, f - 1], kv1_r.at[which, f - 1], flip(f))

    def q_copy(f):
        return remote(q_in.at[flip_batch(f)], qs.at[f], q_sem.at[0, f - 1], q_sem.at[1, f - 1], flip(f))

    def do_copy(f):
        return remote(do_in.at[flip_batch(f)], dos.at[f], do_sem.at[0, f - 1], do_sem.at[1, f - 1], flip(f))

    for f in (1, 2, 3):
        kv1(f, 0).start()
        kv1(f, 1).start()
    for f in (1, 2, 3):
        q_copy(f).start()
    for f in (1, 2, 3):
        do_copy(f).start()

    def kv2(a, f):
        g = flip(f)
        return remote(kv.at[:, g], kv.at[:, g], kv2_s.at[(a - 1) * 4 + f], kv_r.at[g], group(a))

    def kvd(g):
        return remote(kv.at[:, g], kv.at[:, g], kvd_s.at[g // 2], kv_r.at[g], sibling)

    own[0].wait()
    own[1].wait()
    for f in range(4):
        if f:
            kv1(f, 0).wait_recv()
            kv1(f, 1).wait_recv()
        for a in (1, 2, 3):
            kv2(a, f).start()
        kvd(flip(f)).start()

    def member(a, f):
        ax, ay, fx, fy = a % 2, a // 2, f % 2, f // 2
        xa = x + ax * (1 + 4 * qx - 2 * x)
        ya = y + ay * (1 + 4 * qy - 2 * y)
        return ((ya + fy * (3 - 2 * ya)) * side + xa + fx * (3 - 2 * xa)) * 2 + core

    def arrive(i, carry):
        g = member(1 + i % 3, i // 3)
        remote(kv.at[:, g], kv.at[:, g], kvd_s.at[g // 2], kv_r.at[g], sibling).wait_recv()
        kvd(g).start()
        return carry

    lax.fori_loop(0, 12, arrive, 0)

    def arrive_sibling(i, carry):
        g = 2 * i + 1 - core
        remote(kv.at[:, g], kv.at[:, g], kvd_s.at[i], kv_r.at[g], sibling).wait_recv()
        return carry

    lax.fori_loop(0, chunks, arrive_sibling, 0)

    def transpose_rows(src, dst, f):
        for r in range(rows // tile):
            dst[f, :, r * tile:(r + 1) * tile] = src[f, r * tile:(r + 1) * tile, :].T

    def visible(r):
        key = lax.broadcasted_iota(jnp.int32, (keys, tile), 0) - core * tokens
        token = (lax.broadcasted_iota(jnp.int32, (keys, tile), 1) + r * tile) // heads
        return key <= token

    def load_chunk(which, j):
        return kv[which, pl.ds(2 * j, 2)].reshape(keys, head_dim)

    def forward(f, j, masked):
        k_blk = load_chunk(0, j)
        vt_blk = load_chunk(1, j).T
        for r in range(rows // tile):
            cols = slice(r * tile, (r + 1) * tile)
            s = dot(k_blk, qt[f, :, cols]) * alpha
            if masked:
                s = jnp.where(visible(r), s, -jnp.inf)
            m_old = m_s[:, cols]
            m_new = jnp.maximum(m_old, jnp.max(s, axis=0, keepdims=True))
            p = jnp.exp2(s - m_new)
            corr = jnp.exp2(m_old - m_new)
            l_s[:, cols] = l_s[:, cols] * corr + jnp.sum(p, axis=0, keepdims=True)
            m_s[:, cols] = m_new
            ot[:, cols] = ot[:, cols] * corr + dot(vt_blk, p.astype(BF16))

    def o_copy(f):
        return remote(o_st.at[f], out.at[batch], o_sem.at[0, f - 1], o_sem.at[1, f - 1], flip(f))

    def lse_copy(f):
        return remote(lse_st.at[f], lse_out.at[batch], ls_sem.at[0, f - 1], ls_sem.at[1, f - 1], flip(f))

    own_out = [
        pltpu.make_async_copy(o_st.at[0], out.at[batch], loc_sem.at[4]),
        pltpu.make_async_copy(lse_st.at[0], lse_out.at[batch], loc_sem.at[5]),
        pltpu.make_async_copy(dq_st.at[0], dq_out.at[batch], loc_sem.at[6]),
        pltpu.make_async_copy(fin.at[0, 0], dk_out.at[batch], loc_sem.at[7]),
        pltpu.make_async_copy(fin.at[0, 1], dv_out.at[batch], loc_sem.at[8]),
    ]

    def forward_slot(f):
        transpose_rows(qs, qt, f)
        m_s[...] = jnp.full(m_s.shape, -jnp.inf, F32)
        l_s[...] = jnp.zeros(l_s.shape, F32)
        ot[...] = jnp.zeros(ot.shape, F32)
        last = flip(f) // 2

        def body(j, carry):
            forward(f, j, False)
            return carry

        lax.fori_loop(0, last, body, 0)
        forward(f, last, True)
        lse = m_s[...] + jnp.log2(l_s[...])
        lse2[f] = lse
        lse_st[f] = lse * LN2
        for r in range(rows // tile):
            cols = slice(r * tile, (r + 1) * tile)
            low = (ot[:, cols] * (1.0 / l_s[:, cols])).astype(BF16)
            ot_low[f, :, cols] = low
            o_st[f, cols, :] = low.T

    own[2].wait()
    forward_slot(0)
    own_out[0].start()
    own_out[1].start()

    def forward_rest(f, carry):
        q_copy(f).wait_recv()
        forward_slot(f)
        o_copy(f).start()
        lse_copy(f).start()
        return carry

    lax.fori_loop(1, 4, forward_rest, 0)

    def prepare(f):
        transpose_rows(dos, dot_t, f)
        for r in range(rows // tile):
            cols = slice(r * tile, (r + 1) * tile)
            prod = ot_low[f, :, cols].astype(F32) * dot_t[f, :, cols].astype(F32)
            delta[f, :, cols] = jnp.sum(prod, axis=0, keepdims=True)
        dqt[f] = jnp.zeros(dqt.shape[1:], F32)

    own[3].wait()
    prepare(0)

    def prepare_rest(f, carry):
        do_copy(f).wait_recv()
        prepare(f)
        return carry

    lax.fori_loop(1, 4, prepare_rest, 0)

    def backward(f, j, masked):
        k_blk = load_chunk(0, j)
        v_blk = load_chunk(1, j)
        kt_blk = k_blk.T
        for r in range(rows // tile):
            cols = slice(r * tile, (r + 1) * tile)
            s = dot(k_blk, qt[f, :, cols]) * alpha
            p = jnp.exp2(s - lse2[f, :, cols])
            if masked:
                p = jnp.where(visible(r), p, 0.0)
            dp = dot(v_blk, dot_t[f, :, cols])
            ds = p * (dp - delta[f, :, cols])
            p_s[:, cols] = p.astype(BF16)
            ds_s[:, cols] = ds.astype(BF16)
        shape = (2, tokens, head_dim)
        dkdv[1, pl.ds(2 * j, 2)] += dot(p_s[...], dos[f]).reshape(shape)
        dkdv[0, pl.ds(2 * j, 2)] += dot(ds_s[...], qs[f]).reshape(shape)
        for r in range(rows // tile):
            cols = slice(r * tile, (r + 1) * tile)
            dqt[f, :, cols] += dot(kt_blk, ds_s[:, cols])

    def dq_copy(f):
        return remote(dq_st.at[f], dq_out.at[batch], dq_sem.at[0, f - 1], dq_sem.at[1, f - 1], flip(f))

    def finish_dq(f):
        for r in range(rows // tile):
            cols = slice(r * tile, (r + 1) * tile)
            dq_st[f, cols, :] = (dqt[f, :, cols] * scale).astype(BF16).T

        @pl.when(f == 0)
        def _():
            own_out[2].start()

        @pl.when(f > 0)
        def _():
            dq_copy(f).start()

    def r1(j):
        return remote(dkdv.at[:, 2 * j + 1 - core], sib.at[:, j], r1_s.at[j], r1_r.at[j], sibling)

    def r2(g, a, f):
        i = (a - 1) * 4 + f
        return remote(dkdv.at[:, g], peer.at[i], r2_s.at[i], r2_r.at[i], group(a))

    def reduce_chunk(j):
        g = 2 * j + core
        r1(j).wait_recv()
        dkdv[:, g] += sib[:, j]
        xb, yb = j % side, j // side
        bx, by = xb // 2, yb // 2
        vx, vy = xb + bx * (3 - 2 * xb), yb + by * (3 - 2 * yb)
        a = (ux + vx - 2 * ux * vx) + 2 * (uy + vy - 2 * uy * vy)
        f = (qx + bx - 2 * qx * bx) + 2 * (qy + by - 2 * qy * by)

        @pl.when(a > 0)
        def _():
            r2(g, a, f).start()

    def backward_chunk(j, carry):
        dkdv[:, pl.ds(2 * j, 2)] = jnp.zeros((2, 2, tokens, head_dim), F32)

        def slot(f, inner):
            last = flip(f) // 2

            @pl.when(j < last)
            def _():
                backward(f, j, False)

            @pl.when(j == last)
            def _():
                backward(f, j, True)
                finish_dq(f)

            return inner

        lax.fori_loop(0, 4, slot, 0)
        r1(j).start()

        @pl.when(j > 0)
        def _():
            reduce_chunk(j - 1)

        return carry

    lax.fori_loop(0, chunks, backward_chunk, 0)
    reduce_chunk(chunks - 1)

    def fin_copy(f, which):
        dst = (dk_out, dv_out)[which]
        return remote(fin.at[f, which], dst.at[batch], r3_s.at[which, f - 1], r3_r.at[which, f - 1], flip(f))

    def finish_kv(f):
        g = flip(f)
        for a in (1, 2, 3):
            r2(g, a, f).wait_recv()
        total = dkdv[:, g] + peer[f] + peer[4 + f] + peer[8 + f]
        fin[f, 0] = (total[0] * scale).astype(BF16)
        fin[f, 1] = total[1].astype(BF16)

    for f in (1, 2, 3, 0):
        finish_kv(f)
        if f:
            fin_copy(f, 0).start()
            fin_copy(f, 1).start()
        else:
            own_out[3].start()
            own_out[4].start()

    for f in (1, 2, 3):
        for which in (0, 1):
            kv1(f, which).wait_send()
            fin_copy(f, which).wait()
        q_copy(f).wait_send()
        do_copy(f).wait_send()
        o_copy(f).wait()
        lse_copy(f).wait()
        dq_copy(f).wait()
    for copy in own_out:
        copy.wait()

    def drain(i, carry):
        kv2(1 + i // 4, i % 4).wait_send()
        r2(flip(i % 4), 1 + i // 4, i % 4).wait_send()
        return carry

    lax.fori_loop(0, 12, drain, 0)

    def drain_sibling(j, carry):
        kvd(2 * j + core).wait_send()
        r1(j).wait_send()
        return carry

    lax.fori_loop(0, chunks, drain_sibling, 0)


def solution(mesh):
    cp_size = mesh.shape["cp"]

    def attention_shard(queries, keys, values, out_grad):
        batch, tokens, heads, head_dim = queries.shape
        rows = tokens * heads
        q_rows = queries.reshape(batch, rows, head_dim)
        do_rows = out_grad.reshape(batch, rows, head_dim)
        k_rows = keys.reshape(batch, tokens, head_dim)
        v_rows = values.reshape(batch, tokens, head_dim)
        any_spec = pl.BlockSpec(memory_space=pl.ANY)
        dma = pltpu.SemaphoreType.DMA
        block = (tokens, head_dim)
        shapes = [
            jax.ShapeDtypeStruct((batch, rows, head_dim), BF16),
            jax.ShapeDtypeStruct((batch, 1, rows), F32),
            jax.ShapeDtypeStruct((batch, rows, head_dim), BF16),
            jax.ShapeDtypeStruct((batch,) + block, BF16),
            jax.ShapeDtypeStruct((batch,) + block, BF16),
        ]
        scratch = [
            pltpu.VMEM((4, rows, head_dim), BF16),
            pltpu.VMEM((4, rows, head_dim), BF16),
            pltpu.VMEM((4, head_dim, rows), BF16),
            pltpu.VMEM((4, head_dim, rows), BF16),
            pltpu.VMEM((2, cp_size) + block, BF16),
            pltpu.VMEM((head_dim, rows), F32),
            pltpu.VMEM((4, head_dim, rows), BF16),
            pltpu.VMEM((4, rows, head_dim), BF16),
            pltpu.VMEM((1, rows), F32),
            pltpu.VMEM((1, rows), F32),
            pltpu.VMEM((4, 1, rows), F32),
            pltpu.VMEM((4, 1, rows), F32),
            pltpu.VMEM((4, 1, rows), F32),
            pltpu.VMEM((2 * tokens, rows), BF16),
            pltpu.VMEM((2 * tokens, rows), BF16),
            pltpu.VMEM((4, head_dim, rows), F32),
            pltpu.VMEM((4, rows, head_dim), BF16),
            pltpu.VMEM((2, cp_size) + block, F32),
            pltpu.VMEM((2, cp_size // 2) + block, F32),
            pltpu.VMEM((12, 2) + block, F32),
            pltpu.VMEM((4, 2) + block, BF16),
            dma((9,)), dma((2, 3)), dma((2, 3)), dma((12,)), dma((cp_size // 2,)), dma((cp_size,)),
            dma((2, 3)), dma((2, 3)), dma((2, 3)), dma((2, 3)), dma((2, 3)),
            dma((cp_size // 2,)), dma((cp_size // 2,)), dma((12,)), dma((12,)), dma((2, 3)), dma((2, 3)),
        ]
        out, lse, dq, dk, dv = pl.pallas_call(
            attention_kernel,
            out_shape=shapes,
            in_specs=[any_spec] * 4,
            out_specs=[any_spec] * 5,
            scratch_shapes=scratch,
            name="attention",
            compiler_params=pltpu.CompilerParams(
                collective_id=0, has_side_effects=True, vmem_limit_bytes=60 * 1024 * 1024),
        )(q_rows, do_rows, k_rows, v_rows)
        row_lse = jnp.transpose(lse.reshape(batch, tokens, heads), (0, 2, 1))
        return out.reshape(queries.shape), row_lse, dq.reshape(queries.shape), dk.reshape(keys.shape), dv.reshape(values.shape)

    seq_spec = P("dp", "cp")
    return jax.shard_map(attention_shard, mesh=mesh, in_specs=(seq_spec, seq_spec, seq_spec, seq_spec), out_specs=(seq_spec, P("dp", None, "cp"), seq_spec, seq_spec, seq_spec), check_vma=False)
```

time: 1500 us -> 140 us (0.09)
  the two profiles are of different devices: /device:TPU:120 before, /device:TPU:108 now
where the time goes in v1:
time: 140 us
  Pallas kernels  132 us (94%)
  local copies, waits for them, and re-layouts  6.8 us (5%)
    pallas_call x1, Pallas kernels, attention_shard(): pl.pallas_call(attention_kernel, out_shape=shapes, in_specs=[any_spec] *...  132 us
    unnamed x11, local copies, waits for them, and re-layouts  6.64 us

profile of v1, /device:TPU:108, one launch (start us, length us, event | category | flops | bytes accessed | tf_op | source)
XLA Modules:
  0.0 139.9 jit_solution(9914258186325647257)
XLA Ops:
  0.6 131.7 %attention.1 = (bf16[4,1024,256]{2,1,0:T(8,128)(2,1)}, f32[4,1,1024]{2,1,0:T(1,128)}, bf16[4,1024,256]{2,1,0:T(8,128)(2,1)}, bf16[4,128,256]{2,1,0:T(8,128)(2,1)}, bf16[4,128,256]{2,1,0:T(8,128)(2,1)}) custom-call(bf16[4,1024,256]{2,1,0:T(8,128)(2,1)} %bitcast.13, bf16[4,1024,256]{2,1,0:T(8,128)(2,1)} %bitcast.14, bf16[4,128,256]{2,1,0:T(8,128)(2,1)} %bitcast.18, ...), custom_call_target="tpu_custom_call" | custom-call | tf_op jit(solution)/shard_map/attention/pallas_call | solution.py:409
  132.3 0.8 reduce
  133.1 0.2 reshape.42
  133.3 0.7 copy.12
  134.0 0.0 copy-start
  134.0 3.2 %copy.19 = bf16[4,128,8,256]{3,2,1,0:T(8,128)(2,1)} copy(bf16[4,128,8,256]{3,2,1,0:T(8,128)(2,1)} %bitcast.16) | data formatting | bytes 4194304
  137.2 0.0 copy-done
  137.2 0.0 copy-start.2
  137.2 0.0 copy-start.1
  137.2 1.3 copy.20
  138.5 0.0 copy-done.2
  138.5 0.7 copy.21
  139.2 0.0 copy-done.1
  139.2 0.7 copy.22
Async XLA Ops:
  134.0 3.2 %copy-start = (bf16[4,1024,256]{2,1,0:T(8,128)(2,1)S(1)}, bf16[4,1024,256]{2,1,0:T(8,128)(2,1)}, u32[]{:S(2)}) copy-start(bf16[4,1024,256]{2,1,0:T(8,128)(2,1)} %get-tuple-element.12) | copy-start | bytes 6291460
  137.2 1.3 copy-start.2
  137.2 2.0 %copy-start.1 = (bf16[4,128,256]{2,1,0:T(8,128)(2,1)S(1)}, bf16[4,128,256]{2,1,0:T(8,128)(2,1)}, u32[]{:S(2)}) copy-start(bf16[4,128,256]{2,1,0:T(8,128)(2,1)} %get-tuple-element.14) | copy-start | bytes 786436

commit v2 on v1

--- a/solution.py
+++ b/solution.py
@@ -18,10 +18,10 @@
 
 
 def attention_kernel(q_in, do_in, k_in, v_in, out, lse_out, dq_out, dk_out, dv_out,
-                     qs, dos, qt, dot_t, kv, ot, ot_low, o_st, m_s, l_s, lse2, delta, lse_st, p_s, ds_s,
-                     dqt, dq_st, dkdv, sib, peer, fin,
-                     loc_sem, kv1_s, kv1_r, kv2_s, kvd_s, kv_r, q_sem, do_sem, o_sem, ls_sem, dq_sem,
-                     r1_s, r1_r, r2_s, r2_r, r3_s, r3_r):
+                     qs, dos, qt, dot_t, kv, ot, ot_low, o_st, m_s, l_s, lse2, delta, lse_st, bias, s_s, top_s, p_s, ds_s,
+                     dqt, dq_st, dkdv, sib, peer, relay, fin,
+                     loc_sem, kv1_s, kv1_r, kv2_s, kvf_s, kvd_s, kv_r, q_sem, do_sem, o_sem, ls_sem, dq_sem,
+                     r1_s, r1_r, r2_s, r2_r, rl_s, rl_r, r3_s, r3_r, gate):
     tokens, head_dim = k_in.shape[1], k_in.shape[2]
     rows = q_in.shape[1]
     heads = rows // tokens
@@ -86,27 +86,16 @@
     for f in (1, 2, 3):
         kv1(f, 0).start()
         kv1(f, 1).start()
-    for f in (1, 2, 3):
-        q_copy(f).start()
-    for f in (1, 2, 3):
-        do_copy(f).start()
 
     def kv2(a, f):
         g = flip(f)
         return remote(kv.at[:, g], kv.at[:, g], kv2_s.at[(a - 1) * 4 + f], kv_r.at[g], group(a))
 
+    def kvf(g, f, a):
+        return remote(kv.at[:, g], kv.at[:, g], kvf_s.at[f], kv_r.at[g], group(a))
+
     def kvd(g):
         return remote(kv.at[:, g], kv.at[:, g], kvd_s.at[g // 2], kv_r.at[g], sibling)
-
-    own[0].wait()
-    own[1].wait()
-    for f in range(4):
-        if f:
-            kv1(f, 0).wait_recv()
-            kv1(f, 1).wait_recv()
-        for a in (1, 2, 3):
-            kv2(a, f).start()
-        kvd(flip(f)).start()
 
     def member(a, f):
         ax, ay, fx, fy = a % 2, a // 2, f % 2, f // 2
@@ -114,29 +103,9 @@
         ya = y + ay * (1 + 4 * qy - 2 * y)
         return ((ya + fy * (3 - 2 * ya)) * side + xa + fx * (3 - 2 * xa)) * 2 + core
 
-    def arrive(i, carry):
-        g = member(1 + i % 3, i // 3)
-        remote(kv.at[:, g], kv.at[:, g], kvd_s.at[g // 2], kv_r.at[g], sibling).wait_recv()
-        kvd(g).start()
-        return carry
-
-    lax.fori_loop(0, 12, arrive, 0)
-
-    def arrive_sibling(i, carry):
-        g = 2 * i + 1 - core
-        remote(kv.at[:, g], kv.at[:, g], kvd_s.at[i], kv_r.at[g], sibling).wait_recv()
-        return carry
-
-    lax.fori_loop(0, chunks, arrive_sibling, 0)
-
     def transpose_rows(src, dst, f):
         for r in range(rows // tile):
             dst[f, :, r * tile:(r + 1) * tile] = src[f, r * tile:(r + 1) * tile, :].T
-
-    def visible(r):
-        key = lax.broadcasted_iota(jnp.int32, (keys, tile), 0) - core * tokens
-        token = (lax.broadcasted_iota(jnp.int32, (keys, tile), 1) + r * tile) // heads
-        return key <= token
 
     def load_chunk(which, j):
         return kv[which, pl.ds(2 * j, 2)].reshape(keys, head_dim)
@@ -148,14 +117,47 @@
             cols = slice(r * tile, (r + 1) * tile)
             s = dot(k_blk, qt[f, :, cols]) * alpha
             if masked:
-                s = jnp.where(visible(r), s, -jnp.inf)
+                s = s + bias[:, cols]
             m_old = m_s[:, cols]
             m_new = jnp.maximum(m_old, jnp.max(s, axis=0, keepdims=True))
             p = jnp.exp2(s - m_new)
             corr = jnp.exp2(m_old - m_new)
-            l_s[:, cols] = l_s[:, cols] * corr + jnp.sum(p, axis=0, keepdims=True)
+            l_s[:, cols] = l_s[:, cols] * corr + jnp.sum(p.reshape(keys // 8, 8, tile), axis=0)
             m_s[:, cols] = m_new
             ot[:, cols] = ot[:, cols] * corr + dot(vt_blk, p.astype(BF16))
+
+    def scores(f, j, r, k_blk):
+        cols = slice(r * tile, (r + 1) * tile)
+        s = dot(k_blk, qt[f, :, cols])
+        s_s[:, cols] = s
+        top_s[:, cols] = jnp.max(s.reshape(keys // 8, 8, tile), axis=0)
+
+    def scores_all(f, j):
+        k_blk = load_chunk(0, j)
+        for r in range(rows // tile):
+            scores(f, j, r, k_blk)
+
+    def weigh(f, j, masked, ahead):
+        vt_blk = load_chunk(1, j).T
+        k_next = load_chunk(0, j + 1) if ahead else None
+        for r in range(rows // tile):
+            cols = slice(r * tile, (r + 1) * tile)
+            s = s_s[:, cols]
+            if masked:
+                s = s + bias[:, cols]
+                top = jnp.max(s, axis=0, keepdims=True)
+            else:
+                top = jnp.max(top_s[:, cols], axis=0, keepdims=True)
+            m_old = m_s[:, cols]
+            m_new = jnp.maximum(m_old, top * alpha)
+            p = jnp.exp2(s * alpha - m_new)
+            corr = jnp.exp2(m_old - m_new)
+            l_s[:, cols] = l_s[:, cols] * corr + jnp.sum(p.reshape(keys // 8, 8, tile), axis=0)
+            m_s[:, cols] = m_new
+            p_s[:, cols] = p.astype(BF16)
+            if ahead:
+                scores(f, j + 1, r, k_next)
+            ot[:, cols] = ot[:, cols] * corr + dot(vt_blk, p_s[:, cols])
 
     def o_copy(f):
         return remote(o_st.at[f], out.at[batch], o_sem.at[0, f - 1], o_sem.at[1, f - 1], flip(f))
@@ -171,59 +173,133 @@
         pltpu.make_async_copy(fin.at[0, 1], dv_out.at[batch], loc_sem.at[8]),
     ]
 
-    def forward_slot(f):
+    def start_slot(f):
         transpose_rows(qs, qt, f)
         m_s[...] = jnp.full(m_s.shape, -jnp.inf, F32)
         l_s[...] = jnp.zeros(l_s.shape, F32)
         ot[...] = jnp.zeros(ot.shape, F32)
-        last = flip(f) // 2
-
-        def body(j, carry):
-            forward(f, j, False)
-            return carry
-
-        lax.fori_loop(0, last, body, 0)
-        forward(f, last, True)
-        lse = m_s[...] + jnp.log2(l_s[...])
+
+    def finish_slot(f):
+        total = jnp.sum(l_s[...], axis=0, keepdims=True)
+        m_s[...] = m_s[...] + jnp.log2(total)
+        l_s[0:1] = 1.0 / total
+        lse = m_s[...]
         lse2[f] = lse
         lse_st[f] = lse * LN2
         for r in range(rows // tile):
             cols = slice(r * tile, (r + 1) * tile)
-            low = (ot[:, cols] * (1.0 / l_s[:, cols])).astype(BF16)
+            low = (ot[:, cols] * l_s[0:1, cols]).astype(BF16)
             ot_low[f, :, cols] = low
             o_st[f, cols, :] = low.T
 
-    own[2].wait()
-    forward_slot(0)
-    own_out[0].start()
-    own_out[1].start()
-
-    def forward_rest(f, carry):
-        q_copy(f).wait_recv()
-        forward_slot(f)
-        o_copy(f).start()
-        lse_copy(f).start()
-        return carry
-
-    lax.fori_loop(1, 4, forward_rest, 0)
+    def transpose_grad(f):
+        transpose_rows(dos, dot_t, f)
+        dqt[f] = jnp.zeros(dqt.shape[1:], F32)
 
     def prepare(f):
-        transpose_rows(dos, dot_t, f)
+        transpose_grad(f)
         for r in range(rows // tile):
             cols = slice(r * tile, (r + 1) * tile)
             prod = ot_low[f, :, cols].astype(F32) * dot_t[f, :, cols].astype(F32)
             delta[f, :, cols] = jnp.sum(prod, axis=0, keepdims=True)
-        dqt[f] = jnp.zeros(dqt.shape[1:], F32)
-
+
+    own[2].wait()
+    start_slot(0)
+
+    def clear(g, carry):
+        dkdv[:, g] = jnp.zeros((2, tokens, head_dim), F32)
+        return carry
+
+    lax.fori_loop(0, blocks, clear, 0)
+
+    def bias_rows(i, carry):
+        key = lax.broadcasted_iota(jnp.int32, (8, rows), 0) + i * 8 - core * tokens
+        token = lax.broadcasted_iota(jnp.int32, (8, rows), 1) // heads
+        bias[pl.ds(pl.multiple_of(i * 8, 8), 8)] = jnp.where(key <= token, 0.0, -jnp.inf)
+        return carry
+
+    lax.fori_loop(0, keys // 8, bias_rows, 0)
+    own[0].wait()
+    own[1].wait()
+
+    def spread(f):
+        for a in (1, 2):
+            kv2(a, f).start()
+        kvd(flip(f)).start()
+
+    spread(0)
+
+    def spread_rest(f, carry):
+        kv1(f, 0).wait_recv()
+        kv1(f, 1).wait_recv()
+        spread(f)
+        return carry
+
+    lax.fori_loop(1, 4, spread_rest, 0)
+    q_copy(1).start()
+    q_copy(2).start()
+
+    def wait_block(g):
+        remote(kv.at[:, g], kv.at[:, g], kvd_s.at[g // 2], kv_r.at[g], sibling).wait_recv()
+
+    def source(i):
+        late = i // 8
+        return (1 - late) * (1 + i % 2) + 3 * late, (1 - late) * (i // 2) + late * (i - 8)
+
+    def arrive(i):
+        a, f = source(i)
+        g = member(a, f)
+        wait_block(g)
+        kvd(g).start()
+
+        @pl.when(a + (f + f // 2) % 2 == 1)
+        def _():
+            kvf(g, f, 2).start()
+
+        @pl.when((a - 1) * (2 - (f + f // 2) % 2) == 1)
+        def _():
+            kvf(g, f, 1).start()
+
+    def use_chunk(g):
+        wait_block(g + 1 - 2 * core)
+        j = g // 2
+
+        @pl.when(j < me // 2)
+        def _():
+            forward(0, j, False)
+
+        @pl.when(j == me // 2)
+        def _():
+            forward(0, j, True)
+
+    def gather_first(i, carry):
+        arrive(i)
+        use_chunk(flip(i))
+        return carry
+
+    def gather_next(i, carry):
+        @pl.when(i == 6)
+        def _():
+            for f in (1, 2):
+                q_copy(f).wait_send()
+                do_copy(f).start()
+
+        arrive(i)
+        use_chunk(member(*source(i - 4)))
+        return carry
+
+    def gather_last(i, carry):
+        use_chunk(member(*source(i)))
+        return carry
+
+    lax.fori_loop(0, 4, gather_first, 0)
+    lax.fori_loop(4, 12, gather_next, 0)
+    lax.fori_loop(8, 12, gather_last, 0)
+    finish_slot(0)
+    own_out[0].start()
+    own_out[1].start()
     own[3].wait()
     prepare(0)
-
-    def prepare_rest(f, carry):
-        do_copy(f).wait_recv()
-        prepare(f)
-        return carry
-
-    lax.fori_loop(1, 4, prepare_rest, 0)
 
     def backward(f, j, masked):
         k_blk = load_chunk(0, j)
@@ -232,9 +308,9 @@
         for r in range(rows // tile):
             cols = slice(r * tile, (r + 1) * tile)
             s = dot(k_blk, qt[f, :, cols]) * alpha
+            if masked:
+                s = s + bias[:, cols]
             p = jnp.exp2(s - lse2[f, :, cols])
-            if masked:
-                p = jnp.where(visible(r), p, 0.0)
             dp = dot(v_blk, dot_t[f, :, cols])
             ds = p * (dp - delta[f, :, cols])
             p_s[:, cols] = p.astype(BF16)
@@ -254,13 +330,60 @@
             cols = slice(r * tile, (r + 1) * tile)
             dq_st[f, cols, :] = (dqt[f, :, cols] * scale).astype(BF16).T
 
-        @pl.when(f == 0)
-        def _():
-            own_out[2].start()
-
-        @pl.when(f > 0)
-        def _():
-            dq_copy(f).start()
+    def middle_slot(f, carry):
+        last = flip(f) // 2
+
+        q_copy(f).wait_recv()
+
+        @pl.when(f == 3)
+        def _():
+            q_copy(3).wait_send()
+            do_copy(3).wait_send()
+            pl.semaphore_signal(gate, inc=1, device_id={"cp": sibling}, device_id_type=pl.DeviceIdType.MESH)
+            pl.semaphore_wait(gate, 1)
+            for other in (1, 2):
+                o_copy(other).start()
+                lse_copy(other).start()
+            for other in (1, 2):
+                dq_copy(other).start()
+
+        start_slot(f)
+
+        def forward_body(j, inner):
+            weigh(f, j, False, True)
+            return inner
+
+        scores_all(f, 0)
+        lax.fori_loop(0, last, forward_body, 0)
+        weigh(f, last, True, False)
+        finish_slot(f)
+
+        do_copy(f).wait_recv()
+
+        @pl.when(f == 1)
+        def _():
+            do_copy(1).wait_send()
+            do_copy(2).wait_send()
+            q_copy(3).start()
+            do_copy(3).start()
+
+        prepare(f)
+
+        @pl.when(f < 3)
+        def _():
+            def backward_body(j, inner):
+                backward(f, j, False)
+                return inner
+
+            lax.fori_loop(0, last, backward_body, 0)
+            backward(f, last, True)
+            finish_dq(f)
+
+        return carry
+
+    lax.fori_loop(1, 4, middle_slot, 0)
+    o_copy(3).start()
+    lse_copy(3).start()
 
     def r1(j):
         return remote(dkdv.at[:, 2 * j + 1 - core], sib.at[:, j], r1_s.at[j], r1_r.at[j], sibling)
@@ -269,24 +392,43 @@
         i = (a - 1) * 4 + f
         return remote(dkdv.at[:, g], peer.at[i], r2_s.at[i], r2_r.at[i], group(a))
 
-    def reduce_chunk(j):
+    def r2_relay(g, a, f):
+        return remote(dkdv.at[:, g], relay.at[f], rl_s.at[f], rl_r.at[f], group(a))
+
+    def order(t):
+        stage, f = t // 4, t % 4
+        first = (f + f // 2) % 2
+        half, odd = stage // 2, stage % 2
+        a = 3 * (1 - half) * (1 - odd) + (1 + first) * (1 - half) * odd + (2 - first) * half * (1 - odd)
+        return member(a, f) // 2, a, f, first
+
+    def reduce_pair(t):
+        j, a, f, first = order(t)
         g = 2 * j + core
         r1(j).wait_recv()
         dkdv[:, g] += sib[:, j]
-        xb, yb = j % side, j // side
-        bx, by = xb // 2, yb // 2
-        vx, vy = xb + bx * (3 - 2 * xb), yb + by * (3 - 2 * yb)
-        a = (ux + vx - 2 * ux * vx) + 2 * (uy + vy - 2 * uy * vy)
-        f = (qx + bx - 2 * qx * bx) + 2 * (qy + by - 2 * qy * by)
-
-        @pl.when(a > 0)
+
+        @pl.when(t // 4 == 0)
+        def _():
+            r2_relay(g, 1 + first, f).start()
+
+        @pl.when(t // 4 == 1)
         def _():
             r2(g, a, f).start()
 
-    def backward_chunk(j, carry):
-        dkdv[:, pl.ds(2 * j, 2)] = jnp.zeros((2, 2, tokens, head_dim), F32)
-
-        def slot(f, inner):
+    def reduce_group(t, carry):
+        j, a, f, first = order(t)
+        g = 2 * j + core
+        r2_relay(g, a, f).wait_recv()
+        dkdv[:, g] += relay[f]
+        r2(g, a, f).start()
+        return carry
+
+    def final_chunk(t, carry):
+        j = order(t)[0]
+
+        def slot(i, inner):
+            f = 3 * i
             last = flip(f) // 2
 
             @pl.when(j < last)
@@ -296,21 +438,25 @@
             @pl.when(j == last)
             def _():
                 backward(f, j, True)
-                finish_dq(f)
 
             return inner
 
-        lax.fori_loop(0, 4, slot, 0)
+        lax.fori_loop(0, 2, slot, 0)
         r1(j).start()
 
-        @pl.when(j > 0)
-        def _():
-            reduce_chunk(j - 1)
-
-        return carry
-
-    lax.fori_loop(0, chunks, backward_chunk, 0)
-    reduce_chunk(chunks - 1)
+        @pl.when(t > 0)
+        def _():
+            reduce_pair(t - 1)
+
+        return carry
+
+    lax.fori_loop(0, chunks, final_chunk, 0)
+    finish_dq(3)
+    dq_copy(3).start()
+    finish_dq(0)
+    own_out[2].start()
+    reduce_pair(chunks - 1)
+    lax.fori_loop(8, 12, reduce_group, 0)
 
     def fin_copy(f, which):
         dst = (dk_out, dv_out)[which]
@@ -318,9 +464,9 @@
 
     def finish_kv(f):
         g = flip(f)
-        for a in (1, 2, 3):
+        for a in (1, 2):
             r2(g, a, f).wait_recv()
-        total = dkdv[:, g] + peer[f] + peer[4 + f] + peer[8 + f]
+        total = dkdv[:, g] + peer[f] + peer[4 + f]
         fin[f, 0] = (total[0] * scale).astype(BF16)
         fin[f, 1] = total[1].astype(BF16)
 
@@ -337,8 +483,6 @@
         for which in (0, 1):
             kv1(f, which).wait_send()
             fin_copy(f, which).wait()
-        q_copy(f).wait_send()
-        do_copy(f).wait_send()
         o_copy(f).wait()
         lse_copy(f).wait()
         dq_copy(f).wait()
@@ -347,10 +491,14 @@
 
     def drain(i, carry):
         kv2(1 + i // 4, i % 4).wait_send()
-        r2(flip(i % 4), 1 + i // 4, i % 4).wait_send()
-        return carry
-
-    lax.fori_loop(0, 12, drain, 0)
+        return carry
+
+    lax.fori_loop(0, 8, drain, 0)
+    for f in range(4):
+        kvf(flip(f), f, 1).wait_send()
+        r2(flip(f), 1, f).wait_send()
+        r2(flip(f), 2, f).wait_send()
+        r2_relay(flip(f), 1, f).wait_send()
 
     def drain_sibling(j, carry):
         kvd(2 * j + core).wait_send()
@@ -358,6 +506,38 @@
         return carry
 
     lax.fori_loop(0, chunks, drain_sibling, 0)
+
+
+def output_kernel(out_in, lse_in, dq_in, dk_in, dv_in, out, lse, dq, dk, dv, wide, narrow, sem_in, sem_out):
+    batch, rows = lse_in.shape[0], lse_in.shape[2]
+    heads, tokens = lse.shape[1], lse.shape[2]
+    moves = []
+    for i, (src, dst) in enumerate(((out_in, out), (dq_in, dq))):
+        for b in range(batch):
+            moves.append((src.at[b], wide.at[i, b], dst.at[b]))
+    for i, (src, dst) in enumerate(((dk_in, dk), (dv_in, dv))):
+        moves.append((src, narrow.at[i], dst))
+    steps = [(pltpu.make_async_copy(src, mid, sem_in.at[i]), pltpu.make_async_copy(mid, dst, sem_out.at[i]))
+             for i, (src, mid, dst) in enumerate(moves)]
+    for load, _ in steps:
+        load.start()
+    head = lax.broadcasted_iota(jnp.int32, (heads, rows), 0)
+    mine = lax.broadcasted_iota(jnp.int32, (heads, rows), 1) % heads == head
+    token = lax.broadcasted_iota(jnp.int32, (rows, tokens), 1)
+    pick = jnp.where(lax.broadcasted_iota(jnp.int32, (rows, tokens), 0) // heads == token, 1.0, 0.0).astype(BF16)
+    for load, store in steps:
+        load.wait()
+        store.start()
+    for b in range(batch):
+        rest = jnp.where(mine, lse_in[b], 0.0)
+        total = jnp.zeros((heads, tokens), F32)
+        for _ in range(3):
+            part = rest.astype(BF16)
+            total = total + dot(part, pick)
+            rest = rest - part.astype(F32)
+        lse[b] = total
+    for _, store in steps:
+        store.wait()
 
 
 def solution(mesh):
@@ -390,21 +570,26 @@
             pltpu.VMEM((4, head_dim, rows), BF16),
             pltpu.VMEM((4, rows, head_dim), BF16),
             pltpu.VMEM((1, rows), F32),
-            pltpu.VMEM((1, rows), F32),
+            pltpu.VMEM((8, rows), F32),
             pltpu.VMEM((4, 1, rows), F32),
             pltpu.VMEM((4, 1, rows), F32),
             pltpu.VMEM((4, 1, rows), F32),
+            pltpu.VMEM((2 * tokens, rows), F32),
+            pltpu.VMEM((2 * tokens, rows), F32),
+            pltpu.VMEM((8, rows), F32),
             pltpu.VMEM((2 * tokens, rows), BF16),
             pltpu.VMEM((2 * tokens, rows), BF16),
             pltpu.VMEM((4, head_dim, rows), F32),
             pltpu.VMEM((4, rows, head_dim), BF16),
             pltpu.VMEM((2, cp_size) + block, F32),
             pltpu.VMEM((2, cp_size // 2) + block, F32),
-            pltpu.VMEM((12, 2) + block, F32),
+            pltpu.VMEM((8, 2) + block, F32),
+            pltpu.VMEM((4, 2) + block, F32),
             pltpu.VMEM((4, 2) + block, BF16),
-            dma((9,)), dma((2, 3)), dma((2, 3)), dma((12,)), dma((cp_size // 2,)), dma((cp_size,)),
+            dma((9,)), dma((2, 3)), dma((2, 3)), dma((8,)), dma((4,)), dma((cp_size // 2,)), dma((cp_size,)),
             dma((2, 3)), dma((2, 3)), dma((2, 3)), dma((2, 3)), dma((2, 3)),
-            dma((cp_size // 2,)), dma((cp_size // 2,)), dma((12,)), dma((12,)), dma((2, 3)), dma((2, 3)),
+            dma((cp_size // 2,)), dma((cp_size // 2,)), dma((8,)), dma((8,)), dma((4,)), dma((4,)), dma((2, 3)), dma((2, 3)),
+            pltpu.SemaphoreType.REGULAR,
         ]
         out, lse, dq, dk, dv = pl.pallas_call(
             attention_kernel,
@@ -416,7 +601,18 @@
             compiler_params=pltpu.CompilerParams(
                 collective_id=0, has_side_effects=True, vmem_limit_bytes=60 * 1024 * 1024),
         )(q_rows, do_rows, k_rows, v_rows)
-        row_lse = jnp.transpose(lse.reshape(batch, tokens, heads), (0, 2, 1))
+        vmem_spec = pl.BlockSpec(memory_space=pltpu.VMEM)
+        out, row_lse, dq, dk, dv = pl.pallas_call(
+            output_kernel,
+            out_shape=[shapes[0], jax.ShapeDtypeStruct((batch, heads, tokens), F32)] + shapes[2:],
+            in_specs=[any_spec, vmem_spec, any_spec, any_spec, any_spec],
+            out_specs=[any_spec, vmem_spec, any_spec, any_spec, any_spec],
+            scratch_shapes=[
+                pltpu.VMEM((2, batch, rows, head_dim), BF16), pltpu.VMEM((2, batch) + block, BF16),
+                dma((2 * batch + 2,)), dma((2 * batch + 2,))],
+            name="outputs",
+            compiler_params=pltpu.CompilerParams(vmem_limit_bytes=60 * 1024 * 1024),
+        )(out, lse, dq, dk, dv)
         return out.reshape(queries.shape), row_lse, dq.reshape(queries.shape), dk.reshape(keys.shape), dv.reshape(values.shape)
 
     seq_spec = P("dp", "cp")

time: 140 us -> 129 us (0.921)
  the two profiles are of different devices: /device:TPU:108 before, /device:TPU:97 now
where the time goes in v2:
time: 129 us
  Pallas kernels  128 us (99%)
    pallas_call x1, Pallas kernels, attention_shard(): pl.pallas_call(attention_kernel, out_shape=shapes, in_specs=[any_spec] *...  123 us
    pallas_call x1, Pallas kernels, attention_shard(): pl.pallas_call(output_kernel, out_shape=[shapes[0], jax.ShapeDtypeStruct(...  5.39 us

profile of v2, /device:TPU:97, one launch (start us, length us, event | category | flops | bytes accessed | tf_op | source)
XLA Modules:
  0.0 128.6 jit_solution(13473116606896911929)
XLA Ops:
  0.6 122.5 %attention.1 = (bf16[4,1024,256]{2,1,0:T(8,128)(2,1)}, f32[4,1,1024]{2,1,0:T(1,128)}, bf16[4,1024,256]{2,1,0:T(8,128)(2,1)}, bf16[4,128,256]{2,1,0:T(8,128)(2,1)}, bf16[4,128,256]{2,1,0:T(8,128)(2,1)}) custom-call(bf16[4,1024,256]{2,1,0:T(8,128)(2,1)} %bitcast.12, bf16[4,1024,256]{2,1,0:T(8,128)(2,1)} %bitcast.13, bf16[4,128,256]{2,1,0:T(8,128)(2,1)} %bitcast.14, ...), custom_call_target="tpu_custom_call" | custom-call | tf_op jit(solution)/shard_map/attention/pallas_call | solution.py:594
  123.2 5.4 %outputs.1 = (bf16[4,1024,256]{2,1,0:T(8,128)(2,1)}, f32[4,8,128]{2,1,0:T(8,128)}, bf16[4,1024,256]{2,1,0:T(8,128)(2,1)}, bf16[4,128,256]{2,1,0:T(8,128)(2,1)}, bf16[4,128,256]{2,1,0:T(8,128)(2,1)}) custom-call(bf16[4,1024,256]{2,1,0:T(8,128)(2,1)} %get-tuple-element.15.out_in, f32[4,1,1024]{2,1,0:T(1,128)} %get-tuple-element.16.lse_in, ...), custom_call_target="tpu_custom_call" | custom-call | tf_op jit(solution)/shard_map/outputs/pallas_call | solution.py:605

commit v3 on v2

--- a/solution.py
+++ b/solution.py
@@ -86,6 +86,8 @@
     for f in (1, 2, 3):
         kv1(f, 0).start()
         kv1(f, 1).start()
+    q_copy(1).start()
+    q_copy(2).start()
 
     def kv2(a, f):
         g = flip(f)
@@ -236,8 +238,8 @@
         return carry
 
     lax.fori_loop(1, 4, spread_rest, 0)
-    q_copy(1).start()
-    q_copy(2).start()
+    do_copy(1).start()
+    do_copy(2).start()
 
     def wait_block(g):
         remote(kv.at[:, g], kv.at[:, g], kvd_s.at[g // 2], kv_r.at[g], sibling).wait_recv()
@@ -278,12 +280,6 @@
         return carry
 
     def gather_next(i, carry):
-        @pl.when(i == 6)
-        def _():
-            for f in (1, 2):
-                q_copy(f).wait_send()
-                do_copy(f).start()
-
         arrive(i)
         use_chunk(member(*source(i - 4)))
         return carry
@@ -483,6 +479,8 @@
         for which in (0, 1):
             kv1(f, which).wait_send()
             fin_copy(f, which).wait()
+        if f < 3:
+            q_copy(f).wait_send()
         o_copy(f).wait()
         lse_copy(f).wait()
         dq_copy(f).wait()
@@ -508,7 +506,7 @@
     lax.fori_loop(0, chunks, drain_sibling, 0)
 
 
-def output_kernel(out_in, lse_in, dq_in, dk_in, dv_in, out, lse, dq, dk, dv, wide, narrow, sem_in, sem_out):
+def output_kernel(out_in, lse_in, dq_in, dk_in, dv_in, out, lse, dq, dk, dv, wide, narrow, rows_s, lse_s, sem_in, sem_out):
     batch, rows = lse_in.shape[0], lse_in.shape[2]
     heads, tokens = lse.shape[1], lse.shape[2]
     moves = []
@@ -519,23 +517,30 @@
         moves.append((src, narrow.at[i], dst))
     steps = [(pltpu.make_async_copy(src, mid, sem_in.at[i]), pltpu.make_async_copy(mid, dst, sem_out.at[i]))
              for i, (src, mid, dst) in enumerate(moves)]
+    last = len(steps)
+    lse_load = pltpu.make_async_copy(lse_in, rows_s, sem_in.at[last])
+    lse_store = pltpu.make_async_copy(lse_s, lse, sem_out.at[last])
+    lse_load.start()
     for load, _ in steps:
         load.start()
+    lse_load.wait()
     head = lax.broadcasted_iota(jnp.int32, (heads, rows), 0)
     mine = lax.broadcasted_iota(jnp.int32, (heads, rows), 1) % heads == head
     token = lax.broadcasted_iota(jnp.int32, (rows, tokens), 1)
     pick = jnp.where(lax.broadcasted_iota(jnp.int32, (rows, tokens), 0) // heads == token, 1.0, 0.0).astype(BF16)
-    for load, store in steps:
+    rest = jnp.concatenate([jnp.where(mine, rows_s[b], 0.0) for b in range(batch)], axis=0)
+    total = jnp.zeros((batch * heads, tokens), F32)
+    for _ in range(3):
+        part = rest.astype(BF16)
+        total = total + dot(part, pick)
+        rest = rest - part.astype(F32)
+    lse_s[...] = total.reshape(batch, heads, tokens)
+    for i, (load, store) in enumerate(steps):
         load.wait()
         store.start()
-    for b in range(batch):
-        rest = jnp.where(mine, lse_in[b], 0.0)
-        total = jnp.zeros((heads, tokens), F32)
-        for _ in range(3):
-            part = rest.astype(BF16)
-            total = total + dot(part, pick)
-            rest = rest - part.astype(F32)
-        lse[b] = total
+        if i == 3:
+            lse_store.start()
+    lse_store.wait()
     for _, store in steps:
         store.wait()
 
@@ -601,15 +606,15 @@
             compiler_params=pltpu.CompilerParams(
                 collective_id=0, has_side_effects=True, vmem_limit_bytes=60 * 1024 * 1024),
         )(q_rows, do_rows, k_rows, v_rows)
-        vmem_spec = pl.BlockSpec(memory_space=pltpu.VMEM)
         out, row_lse, dq, dk, dv = pl.pallas_call(
             output_kernel,
             out_shape=[shapes[0], jax.ShapeDtypeStruct((batch, heads, tokens), F32)] + shapes[2:],
-            in_specs=[any_spec, vmem_spec, any_spec, any_spec, any_spec],
-            out_specs=[any_spec, vmem_spec, any_spec, any_spec, any_spec],
+            in_specs=[any_spec] * 5,
+            out_specs=[any_spec] * 5,
             scratch_shapes=[
                 pltpu.VMEM((2, batch, rows, head_dim), BF16), pltpu.VMEM((2, batch) + block, BF16),
-                dma((2 * batch + 2,)), dma((2 * batch + 2,))],
+                pltpu.VMEM((batch, 1, rows), F32), pltpu.VMEM((batch, heads, tokens), F32),
+                dma((2 * batch + 3,)), dma((2 * batch + 3,))],
             name="outputs",
             compiler_params=pltpu.CompilerParams(vmem_limit_bytes=60 * 1024 * 1024),
         )(out, lse, dq, dk, dv)

time: 129 us -> 123 us (0.953)
  Pallas kernels: 128 us -> 122 us
    pallas_call x1, Pallas kernels: 123 us -> 118 us  [attention_shard(): pl.pallas_call(attention_kernel, out_shape=shapes, in_specs=[any_spec] *...]
where the time goes in v3:
time: 123 us
  Pallas kernels  122 us (99%)
    pallas_call x1, Pallas kernels, attention_shard(): pl.pallas_call(attention_kernel, out_shape=shapes, in_specs=[any_spec] *...  118 us
    pallas_call x1, Pallas kernels, attention_shard(): pl.pallas_call(output_kernel, out_shape=[shapes[0], jax.ShapeDtypeStruct(...  4.1 us

profile of v3, /device:TPU:97, one launch (start us, length us, event | category | flops | bytes accessed | tf_op | source)
XLA Modules:
  0.0 122.8 jit_solution(15217195439187325508)
XLA Ops:
  0.6 118.1 %attention.1 = (bf16[4,1024,256]{2,1,0:T(8,128)(2,1)}, f32[4,1,1024]{2,1,0:T(1,128)}, bf16[4,1024,256]{2,1,0:T(8,128)(2,1)}, bf16[4,128,256]{2,1,0:T(8,128)(2,1)}, bf16[4,128,256]{2,1,0:T(8,128)(2,1)}) custom-call(bf16[4,1024,256]{2,1,0:T(8,128)(2,1)} %bitcast.12, bf16[4,1024,256]{2,1,0:T(8,128)(2,1)} %bitcast.13, bf16[4,128,256]{2,1,0:T(8,128)(2,1)} %bitcast.14, ...), custom_call_target="tpu_custom_call" | custom-call | tf_op jit(solution)/shard_map/attention/pallas_call | solution.py:599
  118.7 4.1 %outputs.1 = (bf16[4,1024,256]{2,1,0:T(8,128)(2,1)}, f32[4,8,128]{2,1,0:T(8,128)}, bf16[4,1024,256]{2,1,0:T(8,128)(2,1)}, bf16[4,128,256]{2,1,0:T(8,128)(2,1)}, bf16[4,128,256]{2,1,0:T(8,128)(2,1)}) custom-call(bf16[4,1024,256]{2,1,0:T(8,128)(2,1)} %get-tuple-element.15.out_in, f32[4,1,1024]{2,1,0:T(1,128)} %get-tuple-element.16.lse_in, ...), custom_call_target="tpu_custom_call" | custom-call | tf_op jit(solution)/shard_map/outputs/pallas_call | solution.py:609

commit v4 on v3

--- a/solution.py
+++ b/solution.py
@@ -1,4 +1,3 @@
-import functools
 import math
 
 import jax
@@ -28,7 +27,7 @@
     blocks = kv.shape[1]
     chunks = blocks // 2
     keys = 2 * tokens
-    side = 4
+    side = math.isqrt(chunks)
     scale = head_dim ** -0.5
     alpha = scale / LN2
     tile = min(256, rows)
@@ -412,13 +411,16 @@
         def _():
             r2(g, a, f).start()
 
-    def reduce_group(t, carry):
-        j, a, f, first = order(t)
-        g = 2 * j + core
+    def second(f):
+        a = 2 - (f + f // 2) % 2
+        return r2(2 * (member(a, f) // 2) + core, a, f)
+
+    def reduce_group(f):
+        a = 2 - (f + f // 2) % 2
+        g = 2 * (member(a, f) // 2) + core
         r2_relay(g, a, f).wait_recv()
         dkdv[:, g] += relay[f]
-        r2(g, a, f).start()
-        return carry
+        second(f).start()
 
     def final_chunk(t, carry):
         j = order(t)[0]
@@ -452,7 +454,12 @@
     finish_dq(0)
     own_out[2].start()
     reduce_pair(chunks - 1)
-    lax.fori_loop(8, 12, reduce_group, 0)
+    reduce_group(3)
+    reduce_group(1)
+    second(3).wait_send()
+    second(1).wait_send()
+    reduce_group(0)
+    reduce_group(2)
 
     def fin_copy(f, which):
         dst = (dk_out, dv_out)[which]
@@ -466,7 +473,7 @@
         fin[f, 0] = (total[0] * scale).astype(BF16)
         fin[f, 1] = total[1].astype(BF16)
 
-    for f in (1, 2, 3, 0):
+    for f in (3, 1, 2, 0):
         finish_kv(f)
         if f:
             fin_copy(f, 0).start()
@@ -494,8 +501,9 @@
     lax.fori_loop(0, 8, drain, 0)
     for f in range(4):
         kvf(flip(f), f, 1).wait_send()
-        r2(flip(f), 1, f).wait_send()
-        r2(flip(f), 2, f).wait_send()
+        r2(flip(f), 1 + (f + f // 2) % 2, f).wait_send()
+        if f in (0, 2):
+            second(f).wait_send()
         r2_relay(flip(f), 1, f).wait_send()
 
     def drain_sibling(j, carry):

time: 123 us -> 123 us (level)
  no operation moved by 1% of the time
where the time goes in v4:
time: 123 us
  Pallas kernels  122 us (99%)
    pallas_call x1, Pallas kernels, attention_shard(): pl.pallas_call(attention_kernel, out_shape=shapes, in_specs=[any_spec] *...  118 us
    pallas_call x1, Pallas kernels, attention_shard(): pl.pallas_call(output_kernel, out_shape=[shapes[0], jax.ShapeDtypeStruct(...  4.1 us

profile of v4, /device:TPU:97, one launch (start us, length us, event | category | flops | bytes accessed | tf_op | source)
XLA Modules:
  0.0 122.8 jit_solution(11874899197128164256)
XLA Ops:
  0.6 118.1 %attention.1 = (bf16[4,1024,256]{2,1,0:T(8,128)(2,1)}, f32[4,1,1024]{2,1,0:T(1,128)}, bf16[4,1024,256]{2,1,0:T(8,128)(2,1)}, bf16[4,128,256]{2,1,0:T(8,128)(2,1)}, bf16[4,128,256]{2,1,0:T(8,128)(2,1)}) custom-call(bf16[4,1024,256]{2,1,0:T(8,128)(2,1)} %bitcast.12, bf16[4,1024,256]{2,1,0:T(8,128)(2,1)} %bitcast.13, bf16[4,128,256]{2,1,0:T(8,128)(2,1)} %bitcast.14, ...), custom_call_target="tpu_custom_call" | custom-call | tf_op jit(solution)/shard_map/attention/pallas_call | solution.py:607
  118.7 4.1 %outputs.1 = (bf16[4,1024,256]{2,1,0:T(8,128)(2,1)}, f32[4,8,128]{2,1,0:T(8,128)}, bf16[4,1024,256]{2,1,0:T(8,128)(2,1)}, bf16[4,128,256]{2,1,0:T(8,128)(2,1)}, bf16[4,128,256]{2,1,0:T(8,128)(2,1)}) custom-call(bf16[4,1024,256]{2,1,0:T(8,128)(2,1)} %get-tuple-element.15.out_in, f32[4,1,1024]{2,1,0:T(1,128)} %get-tuple-element.16.lse_in, ...), custom_call_target="tpu_custom_call" | custom-call | tf_op jit(solution)/shard_map/outputs/pallas_call | solution.py:617

commit v5 on v4

--- a/solution.py
+++ b/solution.py
@@ -336,11 +336,11 @@
             do_copy(3).wait_send()
             pl.semaphore_signal(gate, inc=1, device_id={"cp": sibling}, device_id_type=pl.DeviceIdType.MESH)
             pl.semaphore_wait(gate, 1)
-            for other in (1, 2):
+            for other in (2, 1):
+                dq_copy(other).start()
+            for other in (2, 1):
                 o_copy(other).start()
                 lse_copy(other).start()
-            for other in (1, 2):
-                dq_copy(other).start()
 
         start_slot(f)
 

time: 123 us -> 123 us (level)
  no operation moved by 1% of the time
where the time goes in v5:
time: 123 us
  Pallas kernels  122 us (99%)
    pallas_call x1, Pallas kernels, attention_shard(): pl.pallas_call(attention_kernel, out_shape=shapes, in_specs=[any_spec] *...  118 us
    pallas_call x1, Pallas kernels, attention_shard(): pl.pallas_call(output_kernel, out_shape=[shapes[0], jax.ShapeDtypeStruct(...  4.1 us

profile of v5, /device:TPU:97, one launch (start us, length us, event | category | flops | bytes accessed | tf_op | source)
XLA Modules:
  0.0 122.8 jit_solution(16487047247132271475)
XLA Ops:
  0.6 118.1 %attention.1 = (bf16[4,1024,256]{2,1,0:T(8,128)(2,1)}, f32[4,1,1024]{2,1,0:T(1,128)}, bf16[4,1024,256]{2,1,0:T(8,128)(2,1)}, bf16[4,128,256]{2,1,0:T(8,128)(2,1)}, bf16[4,128,256]{2,1,0:T(8,128)(2,1)}) custom-call(bf16[4,1024,256]{2,1,0:T(8,128)(2,1)} %bitcast.12, bf16[4,1024,256]{2,1,0:T(8,128)(2,1)} %bitcast.13, bf16[4,128,256]{2,1,0:T(8,128)(2,1)} %bitcast.14, ...), custom_call_target="tpu_custom_call" | custom-call | tf_op jit(solution)/shard_map/attention/pallas_call | solution.py:607
  118.7 4.1 %outputs.1 = (bf16[4,1024,256]{2,1,0:T(8,128)(2,1)}, f32[4,8,128]{2,1,0:T(8,128)}, bf16[4,1024,256]{2,1,0:T(8,128)(2,1)}, bf16[4,128,256]{2,1,0:T(8,128)(2,1)}, bf16[4,128,256]{2,1,0:T(8,128)(2,1)}) custom-call(bf16[4,1024,256]{2,1,0:T(8,128)(2,1)} %get-tuple-element.15.out_in, f32[4,1,1024]{2,1,0:T(1,128)} %get-tuple-element.16.lse_in, ...), custom_call_target="tpu_custom_call" | custom-call | tf_op jit(solution)/shard_map/outputs/pallas_call | solution.py:617
